TPU v7x, 8 devices: a whole 2x2x1 slice. The times are simulated.
8 devices in a mesh: dp: 1 (over z), tp: 2 (over y), ep: 4 (over x, core).
Axes of the slice: x: 2, y: 2, z: 1, core: 2. Of those that a mesh axis runs over, the one named last changes fastest.
Arguments:
- hidden: bfloat16 [256, 2048], P(('dp', 'ep'))
- expert_ids: int32 [256, 8], P(('dp', 'ep'))
- norm_w: bfloat16 [2048], replicated
- router_w: bfloat16 [2048, 128], replicated
- w_gate: bfloat16 [128, 2048, 768], P('ep', None, 'tp')
- w_up: bfloat16 [128, 2048, 768], P('ep', None, 'tp')
- w_down: bfloat16 [128, 768, 2048], P('ep', 'tp')
Outputs:
- output: bfloat16 [256, 2048], P(('dp', 'ep'))
All inputs are finite; a program needn't handle non-finite values.
Results may differ from a plain program's by a relative error of at most 0.00964266.
Values are sent between devices in bfloat16 or wider.
A program may use at most 1 GiB of HBM per device.

v0:
```python
import jax
import jax.numpy as jnp
from jax import lax
from jax.sharding import PartitionSpec as P

NORM_EPS = 1e-6


def rms_norm(hidden, norm_w):
    wide_h = hidden.astype(jnp.float32)
    mean_sq = jnp.mean(wide_h * wide_h, axis=-1, keepdims=True)
    return (wide_h * lax.rsqrt(mean_sq + NORM_EPS) * norm_w.astype(jnp.float32)).astype(jnp.bfloat16)


def slot_rank(expert_ids, n_experts):
    flat_ids = expert_ids.reshape(-1)
    one_hot = (flat_ids[:, None] == jnp.arange(n_experts, dtype=jnp.int32)[None, :]).astype(jnp.int32)
    running = jnp.cumsum(one_hot, axis=0)
    return jnp.sum(running * one_hot, axis=1) - 1


def row_cap(tok_dev, top_k, n_experts):
    return 8 * ((2 * top_k * tok_dev + 8 * n_experts - 1) // (8 * n_experts))


def gather_slots(normed, slot_dest, n_slots, top_k):
    pair_tok = jnp.arange(slot_dest.shape[0], dtype=jnp.int32) // top_k
    src_tok = jnp.zeros((n_slots,), jnp.int32).at[slot_dest].set(pair_tok)
    filled = jnp.zeros((n_slots,), jnp.int32).at[slot_dest].set(1)
    return jnp.where(filled[:, None] > 0, normed[src_tok], jnp.zeros((), jnp.bfloat16))


def solution(mesh):
    ep_size = mesh.shape["ep"]

    def per_device(hidden, expert_ids, norm_w, router_w, w_gate, w_up, w_down):
        tok_dev, model_dim = hidden.shape
        top_k = expert_ids.shape[1]
        n_experts = router_w.shape[1]
        local_exp = w_gate.shape[0]
        row_limit = row_cap(tok_dev, top_k, n_experts)
        n_slots = n_experts * row_limit
        normed = rms_norm(hidden, norm_w)
        logits = jnp.dot(normed, router_w, preferred_element_type=jnp.float32)
        gate_prob = jnp.take_along_axis(jax.nn.softmax(logits, axis=-1), expert_ids, axis=-1)
        slot_dest = expert_ids.reshape(-1) * row_limit + slot_rank(expert_ids, n_experts)
        send_rows = gather_slots(normed, slot_dest, n_slots, top_k).reshape(ep_size, local_exp, row_limit, model_dim)
        recv_rows = lax.all_to_all(send_rows, "ep", 0, 2, tiled=True).reshape(local_exp, ep_size * row_limit, model_dim)
        gate_pre = jnp.einsum("erd,edf->erf", recv_rows, w_gate, preferred_element_type=jnp.float32)
        up_pre = jnp.einsum("erd,edf->erf", recv_rows, w_up, preferred_element_type=jnp.float32)
        act_rows = (jax.nn.silu(gate_pre) * up_pre).astype(jnp.bfloat16)
        part_out = jnp.einsum("erf,efd->erd", act_rows, w_down, preferred_element_type=jnp.float32).astype(jnp.bfloat16)
        expert_out = lax.psum(part_out, "tp")
        back_rows = lax.all_to_all(expert_out.reshape(1, local_exp, ep_size * row_limit, model_dim), "ep", 2, 0, tiled=True)
        picked = back_rows.reshape(n_slots, model_dim)[slot_dest].reshape(tok_dev, top_k, model_dim)
        moe_sum = jnp.sum(picked.astype(jnp.float32) * gate_prob[:, :, None], axis=1)
        return (hidden.astype(jnp.float32) + moe_sum).astype(jnp.bfloat16)

    token_spec = P(("dp", "ep"), None)
    return jax.shard_map(per_device, mesh=mesh, in_specs=(token_spec, token_spec, P(None), P(None, None), P("ep", None, "tp"), P("ep", None, "tp"), P("ep", "tp", None)), out_specs=token_spec, check_vma=False)
```

profile of v0, /device:TPU:0, one launch (start us, length us, event | category | flops | bytes accessed | tf_op | source)
XLA Modules:
  0.0 322.5 jit_solution(4408428035163907769)
XLA Ops:
  6.5 0.7 broadcast_multiply_fusion
  7.3 0.8 copy.38
  8.1 0.1 eq.29
  8.2 1.1 fusion.12
  9.4 0.7 convert_element_type.32
  10.1 0.1 mul.55
  10.2 0.1 copy.40
  10.4 0.2 fusion.17
  10.7 0.2 fusion.16
  10.9 2.4 scatter_custom_fusion.1
  13.4 2.4 scatter_custom_fusion
  15.9 0.1 broadcast_in_dim.20
  16.0 1.1 fusion.14
  17.1 6.0 %gather_fusion = bf16[1024,2048]{1,0:T(8,128)(2,1)} fusion(bf16[64,2048]{1,0:T(8,128)(2,1)S(1)} %fusion.14, s32[1024]{0:T(1024)S(1)} %fusion.22), kind=kCustom, calls=%fused_computation | custom fusion | bytes 8392704 | tf_op jit(solution)/shard_map/gather | solution.py:30
  23.1 2.5 broadcast_select_fusion
  25.6 52.7 %all_to_all.30 = bf16[4,32,8,2048]{3,2,1,0:T(8,128)(2,1)} all-to-all(bf16[4,32,8,2048]{3,2,1,0:T(8,128)(2,1)S(1)} %broadcast_select_fusion), channel_id=1, replica_groups=mesh['dp'=1,'tp'=2,'ep'=4] {'ep'}, dimensions={0} | all-to-all | bytes 8388608 | tf_op jit(solution)/shard_map/all_to_all | solution.py:48
  78.3 19.5 %fusion.1 = f32[32,32,384]{2,1,0:T(8,128)S(1)} fusion(bf16[32,2048,384]{2,1,0:T(8,128)(2,1)} %param.12, bf16[4,32,8,2048]{3,2,1,0:T(8,128)(2,1)} %all_to_all.30), kind=kOutput, calls=%fused_computation.7 | convolution fusion | flops 1610612736 | bytes 56098816 | tf_op jit(solution)/shard_map/erd,edf->erf/dot_general | solution.py:50
  97.8 19.5 %multiply_convert_fusion.clone.4 = bf16[32,32,384]{2,1,0:T(8,128)(2,1)S(1)} fusion(f32[32,32,384]{2,1,0:T(8,128)S(1)} %fusion.1, bf16[32,2048,384]{2,1,0:T(8,128)(2,1)} %param.11, bf16[4,32,8,2048]{3,2,1,0:T(8,128)(2,1)} %all_to_all.30), kind=kOutput, calls=%fused_computation.15.clone.clone.clone.1 | convolution fusion | flops 1612972032 | bytes 56885248 | tf_op jit(solution)/shard_map/erd,edf->erf/dot_general | solution.py:49
  117.3 19.7 %convert_bitcast_fusion = bf16[1,32,32,2048]{3,2,1,0:T(8,128)(2,1)} fusion(bf16[32,384,2048]{2,1,0:T(8,128)(2,1)} %param.13, bf16[32,32,384]{2,1,0:T(8,128)(2,1)S(1)} %multiply_convert_fusion.clone.4), kind=kOutput, calls=%fused_computation.11 | convolution fusion | flops 1612709888 | bytes 55312384 | tf_op jit(solution)/shard_map/erf,efd->erd/dot_general | solution.py:52
  137.1 102.9 %all-reduce.2.cloned.1.call-done = bf16[1,32,32,2048]{3,2,1,0:T(8,128)(2,1)} async-done(((bf16[1,32,32,2048]{3,2,1,0:T(8,128)(2,1)}), bf16[1,32,32,2048]{3,2,1,0:T(8,128)(2,1)}) %all-reduce.2.cloned.1.call-update) | async-done | bytes 4194320 | tf_op jit(solution)/shard_map/psum | solution.py:53
  240.0 6.5 %copy.43 = bf16[1,32,32,2048]{3,1,0,2:T(8,128)(2,1)} copy(bf16[1,32,32,2048]{3,2,1,0:T(8,128)(2,1)} %all-reduce.2.cloned.1.call-done) | data formatting | bytes 8388608 | tf_op jit(solution)/shard_map/psum | solution.py:53
  246.4 5.2 %all-to-all-start.1 = ((bf16[1,32,32,2048]{3,1,0,2:T(8,128)(2,1)}), bf16[1,32,32,2048]{3,1,0,2:T(8,128)(2,1)}, u32[]{:S(2)}, u32[]{:S(2)}) async-start(bf16[1,32,32,2048]{3,1,0,2:T(8,128)(2,1)} %copy.43), calls=%async_computation.1 | async-start | bytes 8388608 | tf_op jit(solution)/shard_map/all_to_all | solution.py:54
  251.8 0.1 reshape.118
  251.9 0.3 fusion.31
  252.2 0.2 fusion.21
  252.4 0.1 fusion.20
  252.5 3.6 %gather_fusion.2 = f32[512]{0:T(512)S(1)} fusion(f32[64,128]{1,0:T(8,128)S(1)} %fusion.20, s32[512]{0:T(512)S(1)} %reshape.118), kind=kCustom, calls=%fused_computation.2 | custom fusion | bytes 8192 | tf_op jit(solution)/shard_map/jit(take_along_axis)/gather | solution.py:45
  256.4 42.9 %all-to-all-done.1 = bf16[1,32,32,2048]{3,1,0,2:T(8,128)(2,1)} async-done(((bf16[1,32,32,2048]{3,1,0,2:T(8,128)(2,1)}), bf16[1,32,32,2048]{3,1,0,2:T(8,128)(2,1)}, u32[]{:S(2)}, u32[]{:S(2)}) %all-to-all-start.1) | async-done | bytes 4194336 | tf_op jit(solution)/shard_map/all_to_all | solution.py:54
  299.3 6.5 %copy.44 = bf16[1,32,4,8,2048]{4,3,1,2,0:T(8,128)(2,1)} copy(bf16[1,32,4,8,2048]{4,1,3,2,0:T(8,128)(2,1)} %bitcast.10) | data formatting | bytes 8388608 | tf_op jit(solution)/shard_map/all_to_all | solution.py:54
  305.8 7.2 %gather_fusion.1 = bf16[512,2048]{1,0:T(8,128)(2,1)S(1)} fusion(bf16[1024,2048]{1,0:T(8,128)(2,1)} %bitcast.65, s32[1024]{0:T(1024)S(1)} %pad_clamp_fusion), kind=kCustom, calls=%fused_computation.1 | custom fusion | bytes 4196352 | tf_op jit(solution)/shard_map/gather | solution.py:55
  313.0 1.8 fusion
  314.9 0.8 fusion.15
  (30 shorter events, 0.7 us)
Async XLA Ops:
  6.5 245.3 %copy-start = (bf16[2048,128]{1,0:T(8,128)(2,1)S(1)}, bf16[2048,128]{1,0:T(8,128)(2,1)}, u32[]{:S(2)}) copy-start(bf16[2048,128]{1,0:T(8,128)(2,1)} %param.10) | copy-start | bytes 1572868
  6.5 233.4 %all-reduce.2.cloned.1.call-start = ((), (), s32[]{:S(2)}) async-start(), calls=%async_computation.2 | async-start | bytes 8388608 | tf_op jit(solution)/shard_map/psum | solution.py:53
  246.4 5.2 %copy-start.2 = (s32[64,8]{0,1:T(8,128)S(1)}, s32[64,8]{0,1:T(8,128)}, u32[]{:S(2)}) copy-start(s32[64,8]{0,1:T(8,128)} %param.8) | copy-start | bytes 6148
  246.4 52.9 %all-to-all-start.1 = ((bf16[1,32,32,2048]{3,1,0,2:T(8,128)(2,1)}), bf16[1,32,32,2048]{3,1,0,2:T(8,128)(2,1)}, u32[]{:S(2)}, u32[]{:S(2)}) async-start(bf16[1,32,32,2048]{3,1,0,2:T(8,128)(2,1)} %copy.43), calls=%async_computation.1 | async-start | bytes 8388608 | tf_op jit(solution)/shard_map/all_to_all | solution.py:54
  305.8 9.0 %copy-start.1 = (bf16[64,2048]{1,0:T(8,128)(2,1)S(1)}, bf16[64,2048]{1,0:T(8,128)(2,1)}, u32[]{:S(2)}) copy-start(bf16[64,2048]{1,0:T(8,128)(2,1)} %param.7) | copy-start | bytes 786436
Sparse Core Ops, SparseCore 0:
  137.2 102.7 all-reduce.1
where the time goes:
time: 323 us; the launch traced here: 322 us
  waiting for transfers between devices  146 us (45%)
  matrix products  59 us (18%)
  blocking collectives  52.7 us (16%)
  local copies, waits for them, and re-layouts  36.5 us (11%)
  between operations  13.6 us (4%)
  other arithmetic  9.62 us (3%)
  starting transfers between devices  5.21 us (2%)
    psum x1, waiting for transfers between devices, per_device(): expert_out = lax.psum(part_out, 'tp')  103 us
    all_to_all x1, blocking collectives, per_device(): lax.all_to_all(send_rows, 'ep', 0, 2, tiled=True)  52.7 us
    all_to_all x1, waiting for transfers between devices, per_device(): lax.all_to_all(expert_out.reshape(1, local_exp, ep_size * row_limit, mode...  42.9 us
    dot_general x1, matrix products, per_device(): jnp.einsum('erf,efd->erd', act_rows, w_down, preferred_element_type=jnp.f...  19.7 us
    dot_general x1, matrix products, per_device(): jnp.einsum('erd,edf->erf', recv_rows, w_gate, preferred_element_type=jnp....  19.5 us
    dot_general x1, matrix products, per_device(): jnp.einsum('erd,edf->erf', recv_rows, w_up, preferred_element_type=jnp.fl...  19.5 us
    gather x1, local copies, waits for them, and re-layouts, per_device(): back_rows.reshape(n_slots, model_dim)[slot_dest]  7.18 us
    all_to_all x1, local copies, waits for them, and re-layouts, per_device(): lax.all_to_all(expert_out.reshape(1, local_exp, ep_size * row_limit, mode...  6.51 us
  transfers between devices with their start and end apart: 2, of which 2 were waited for; matrix products, arithmetic and copies ran while one was open for 1% of the time, Pallas kernels for 0%

commit v1 on v0

v1 whole, which is shorter than its diff:
```python
import functools

import jax
import jax.numpy as jnp
from jax import lax
from jax.experimental import pallas as pl
from jax.experimental.pallas import tpu as pltpu
from jax.sharding import PartitionSpec as P

NORM_EPS = 1e-6
RING = 10
BLK = 256
F32 = jnp.float32
BF16 = jnp.bfloat16


def row_cap(tok_dev, top_k, n_experts):
    return 8 * ((2 * top_k * tok_dev + 8 * n_experts - 1) // (8 * n_experts))


def moe_kernel(dims, h_hbm, ids_hbm, nw_hbm, rw_hbm, wg_hbm, wu_hbm, wd_hbm, out_hbm,
               ring, wdb, hbuf, idb, nwb, rwb, vbuf, xbuf, posb, cbuf, abuf, ybuf,
               sbuf, ra, tb, rb, zb, rc, obuf,
               gsem, usem, dsem, lsem, hs_sem, hr_sem, is_sem, ir_sem,
               as_sem, ar_sem, bs_sem, br_sem, cs_sem, cr_sem, osem):
    tok, top_k, n_exp, local, ff, d, cap = dims
    n_tok = 4 * tok
    slot_rows = 4 * cap
    n_slots = local * slot_rows
    n_blk = d // BLK
    tp = lax.axis_index("tp")
    ep = lax.axis_index("ep")
    x = ep // 2
    core = ep % 2
    partner = {"ep": x * 2 + (1 - core)}
    across = {"ep": (1 - x) * 2 + core}
    other = {"tp": 1 - tp}
    MESH = pl.DeviceIdType.MESH
    q_own = core * 2 + x
    q_across = core * 2 + (1 - x)
    q_partner = (1 - core) * 2 + x
    q_diag = (1 - core) * 2 + (1 - x)

    def w_copies(e, slot):
        return (
            pltpu.make_async_copy(wg_hbm.at[e], ring.at[slot, :, pl.ds(0, ff)], gsem.at[slot]),
            pltpu.make_async_copy(wu_hbm.at[e], ring.at[slot, :, pl.ds(ff, ff)], usem.at[slot]),
        )

    parts = 4
    per = local // parts

    def d_copy(c, s, k):
        return pltpu.make_async_copy(
            wd_hbm.at[pl.ds(k * per, per), :, pl.ds(pl.multiple_of(c * BLK, BLK), BLK)],
            wdb.at[s, pl.ds(k * per, per)], dsem.at[s, k])

    own_h = pltpu.make_async_copy(h_hbm, hbuf.at[q_own], lsem.at[0])
    own_i = pltpu.make_async_copy(ids_hbm, idb.at[q_own], lsem.at[1])
    nw_c = pltpu.make_async_copy(nw_hbm, nwb, lsem.at[2])
    rw_c = pltpu.make_async_copy(rw_hbm, rwb, lsem.at[3])
    for cp in (own_h, own_i, nw_c, rw_c):
        cp.start()
    for e in range(RING):
        for cp in w_copies(e, e):
            cp.start()
    for c in range(2):
        for k in range(parts):
            d_copy(c, c, k).start()

    barrier = pltpu.get_barrier_semaphore()
    for dev in (partner, across, other):
        pl.semaphore_signal(barrier, inc=1, device_id=dev, device_id_type=MESH)
    pl.semaphore_wait(barrier, 3)

    def h_copy(src, q, dev, n):
        return pltpu.make_async_remote_copy(
            src_ref=src, dst_ref=hbuf.at[q], send_sem=hs_sem.at[n], recv_sem=hr_sem.at[n],
            device_id=dev, device_id_type=MESH)

    def i_copy(src, q, dev, n):
        return pltpu.make_async_remote_copy(
            src_ref=src, dst_ref=idb.at[q], send_sem=is_sem.at[n], recv_sem=ir_sem.at[n],
            device_id=dev, device_id_type=MESH)

    i_x = i_copy(ids_hbm, q_own, across, 0)
    i_p = i_copy(ids_hbm, q_own, partner, 1)
    h_x = h_copy(h_hbm, q_own, across, 0)
    h_p = h_copy(h_hbm, q_own, partner, 1)
    i_x.start()
    i_p.start()
    h_x.start()
    h_p.start()
    i_copy(ids_hbm, q_across, across, 0).wait_recv()
    i_r = i_copy(idb.at[q_across], q_across, partner, 2)
    i_r.start()

    own_i.wait()
    i_copy(ids_hbm, q_partner, partner, 1).wait_recv()
    i_copy(idb.at[q_diag], q_diag, partner, 2).wait_recv()
    ids_t = jnp.concatenate([idb[q] for q in range(4)], axis=1)
    exp_iota = lax.broadcasted_iota(jnp.int32, (n_exp, n_tok), 0)
    member = jnp.zeros((n_exp, n_tok), F32)
    for j in range(top_k):
        member = member + jnp.where(ids_t[j:j + 1, :] == exp_iota, 1.0, 0.0)
    row_i = lax.broadcasted_iota(jnp.int32, (n_tok, n_tok), 0)
    col_i = lax.broadcasted_iota(jnp.int32, (n_tok, n_tok), 1)
    before = jnp.where(row_i < col_i, 1.0, 0.0).astype(BF16)
    pos = jnp.dot(member.astype(BF16), before, preferred_element_type=F32)
    pos = jnp.where(member > 0.5, pos, -1.0)
    posb[...] = pos

    nw_c.wait()

    def norm_rows(q):
        wide = hbuf[q].astype(F32)
        inv = lax.rsqrt(jnp.mean(wide * wide, axis=-1, keepdims=True) + NORM_EPS)
        for k in range(d // 128):
            cols = pl.ds(k * 128, 128)
            part = hbuf[q, :, cols].astype(F32) * inv * nwb[k:k + 1, :].astype(F32)
            vbuf[pl.ds(pl.multiple_of(q * tok, tok), tok), cols] = part.astype(BF16)

    own_h.wait()
    norm_rows(q_own)
    h_copy(h_hbm, q_partner, partner, 1).wait_recv()
    norm_rows(q_partner)
    h_copy(h_hbm, q_across, across, 0).wait_recv()
    h_r = h_copy(hbuf.at[q_across], q_across, partner, 2)
    h_r.start()
    norm_rows(q_across)
    h_copy(hbuf.at[q_diag], q_diag, partner, 2).wait_recv()
    norm_rows(q_diag)

    pos_loc = posb[pl.ds(pl.multiple_of(ep * local, local), local), :]
    slot_f = lax.broadcasted_iota(jnp.int32, (slot_rows, n_tok), 0).astype(F32)
    pick = jnp.concatenate(
        [jnp.where(pos_loc[e:e + 1, :] == slot_f, 1.0, 0.0).astype(BF16) for e in range(local)], axis=0)

    def gather_cols(n, carry):
        cols = pl.ds(pl.multiple_of(n * 256, 256), 256)
        v_cols = vbuf[:, cols]
        for m in range(n_slots // 256):
            rows = jnp.dot(pick[m * 256:(m + 1) * 256], v_cols, preferred_element_type=F32)
            xbuf[m * 256:(m + 1) * 256, cols] = rows.astype(BF16)
        return carry

    lax.fori_loop(0, d // 256, gather_cols, 0)

    def gate_up(e, carry):
        slot = lax.rem(e, RING)
        rows = pl.ds(pl.multiple_of(e * slot_rows, slot_rows), slot_rows)
        for cp in w_copies(e, slot):
            cp.wait()
        pre = jnp.dot(xbuf[rows, :], ring[slot], preferred_element_type=F32)
        gate, up = pre[:, :ff], pre[:, ff:]
        abuf[rows, :] = (gate * jax.nn.sigmoid(gate) * up).astype(BF16)

        @pl.when(e + RING < local)
        def _():
            for cp in w_copies(e + RING, slot):
                cp.start()
        return carry

    lax.fori_loop(0, local, gate_up, 0)

    rw_c.wait()
    logits = jnp.dot(vbuf[...], rwb[...], preferred_element_type=F32)
    expo = jnp.exp(logits - jnp.max(logits, axis=-1, keepdims=True))
    prob = expo / jnp.sum(expo, axis=-1, keepdims=True)
    g_hi = prob.astype(BF16)
    rest = prob - g_hi.astype(F32)
    g_mid = rest.astype(BF16)
    g_lo = (rest - g_mid.astype(F32)).astype(BF16)
    pos_t = posb[...].T.astype(BF16)
    for n in range(n_slots // 256):
        lane = lax.broadcasted_iota(jnp.int32, (n_exp, 256), 1) + n * 256
        sub = lax.broadcasted_iota(jnp.int32, (n_exp, 256), 0)
        spread = jnp.where(sub == ep * local + lane // slot_rows, 1.0, 0.0).astype(BF16)
        want = (lax.broadcasted_iota(jnp.int32, (n_tok, 256), 1) % slot_rows).astype(F32)
        hit = jnp.dot(pos_t, spread, preferred_element_type=F32) == want
        for i, g in enumerate((g_hi, g_mid, g_lo)):
            wide_g = jnp.dot(g, spread, preferred_element_type=F32)
            cbuf[i, :, n * 256:(n + 1) * 256] = jnp.where(hit, wide_g, 0.0).astype(BF16)

    half = n_tok // 2

    def a_copy(c, row):
        return pltpu.make_async_remote_copy(
            src_ref=sbuf.at[c, pl.ds(pl.multiple_of(row * half, half), half)], dst_ref=ra.at[c],
            send_sem=as_sem.at[c], recv_sem=ar_sem.at[c], device_id=partner, device_id_type=MESH)

    def b_copy(c):
        return pltpu.make_async_remote_copy(
            src_ref=tb.at[c, pl.ds(pl.multiple_of((1 - x) * tok, tok), tok)], dst_ref=rb.at[c],
            send_sem=bs_sem.at[c], recv_sem=br_sem.at[c], device_id=across, device_id_type=MESH)

    def c_copy(c):
        return pltpu.make_async_remote_copy(
            src_ref=zb.at[c], dst_ref=rc.at[c],
            send_sem=cs_sem.at[c], recv_sem=cr_sem.at[c], device_id=other, device_id_type=MESH)

    def o_copy(c):
        cols = pl.ds(pl.multiple_of(c * BLK, BLK), BLK)
        return pltpu.make_async_copy(obuf.at[:, cols], out_hbm.at[:, cols], osem.at[c])

    def stage_b(c):
        a_copy(c, 1 - core).wait_recv()
        tb[c] = sbuf[c, pl.ds(pl.multiple_of(core * half, half), half), :] + ra[c]
        b_copy(c).start()

    def stage_c(c):
        b_copy(c).wait_recv()
        zb[c] = tb[c, pl.ds(pl.multiple_of(x * tok, tok), tok), :] + rb[c]
        c_copy(c).start()

    def stage_d(c):
        c_copy(c).wait_recv()
        cols = pl.ds(pl.multiple_of(c * BLK, BLK), BLK)
        obuf[:, cols] = (hbuf[q_own, :, cols].astype(F32) + (zb[c] + rc[c])).astype(BF16)
        o_copy(c).start()

    LAG_B, LAG_C, LAG_D = 1, 3, 5

    def down(c, carry):
        s = lax.rem(c, 2)
        for k in range(parts):
            d_copy(c, s, k).wait()

        def one(e, inner):
            rows = pl.ds(pl.multiple_of(e * slot_rows, slot_rows), slot_rows)
            y = jnp.dot(abuf[rows, :], wdb[s, e], preferred_element_type=F32)
            ybuf[rows, :] = y.astype(BF16)
            return inner

        lax.fori_loop(0, local, one, 0)

        @pl.when(c + 2 < n_blk)
        def _():
            for k in range(parts):
                d_copy(c + 2, s, k).start()

        y_all = ybuf[...]
        total = jnp.dot(cbuf[2], y_all, preferred_element_type=F32)
        total = total + jnp.dot(cbuf[1], y_all, preferred_element_type=F32)
        total = total + jnp.dot(cbuf[0], y_all, preferred_element_type=F32)
        sbuf[c] = total
        a_copy(c, 1 - core).start()

        @pl.when(c >= LAG_B)
        def _():
            stage_b(c - LAG_B)

        @pl.when(c >= LAG_C)
        def _():
            stage_c(c - LAG_C)

        @pl.when(c >= LAG_D)
        def _():
            stage_d(c - LAG_D)
        return carry

    lax.fori_loop(0, n_blk, down, 0)
    for c in range(n_blk - LAG_B, n_blk):
        stage_b(c)
    for c in range(n_blk - LAG_C, n_blk):
        stage_c(c)
    for c in range(n_blk - LAG_D, n_blk):
        stage_d(c)

    for cp in (i_x, i_p, i_r, h_x, h_p, h_r):
        cp.wait_send()

    def drain(c, carry):
        a_copy(c, 1 - core).wait_send()
        b_copy(c).wait_send()
        c_copy(c).wait_send()
        o_copy(c).wait()
        return carry

    lax.fori_loop(0, n_blk, drain, 0)


def solution(mesh):
    def per_device(hidden, expert_ids, norm_w, router_w, w_gate, w_up, w_down):
        tok, d = hidden.shape
        top_k = expert_ids.shape[1]
        n_exp = router_w.shape[1]
        local, _, ff = w_gate.shape
        cap = row_cap(tok, top_k, n_exp)
        dims = (tok, top_k, n_exp, local, ff, d, cap)
        n_tok = 4 * tok
        n_slots = local * 4 * cap
        n_blk = d // BLK
        any_spec = pl.BlockSpec(memory_space=pl.ANY)
        dma = pltpu.SemaphoreType.DMA
        return pl.pallas_call(
            functools.partial(moe_kernel, dims),
            out_shape=jax.ShapeDtypeStruct((tok, d), BF16),
            in_specs=[any_spec] * 7,
            out_specs=any_spec,
            scratch_shapes=[
                pltpu.VMEM((RING, d, 2 * ff), BF16),
                pltpu.VMEM((2, local, ff, BLK), BF16),
                pltpu.VMEM((4, tok, d), BF16),
                pltpu.VMEM((4, top_k, tok), jnp.int32),
                pltpu.VMEM((d // 128, 128), BF16),
                pltpu.VMEM((d, n_exp), BF16),
                pltpu.VMEM((n_tok, d), BF16),
                pltpu.VMEM((n_slots, d), BF16),
                pltpu.VMEM((n_exp, n_tok), F32),
                pltpu.VMEM((3, n_tok, n_slots), BF16),
                pltpu.VMEM((n_slots, ff), BF16),
                pltpu.VMEM((n_slots, BLK), BF16),
                pltpu.VMEM((n_blk, n_tok, BLK), F32),
                pltpu.VMEM((n_blk, n_tok // 2, BLK), F32),
                pltpu.VMEM((n_blk, n_tok // 2, BLK), F32),
                pltpu.VMEM((n_blk, tok, BLK), F32),
                pltpu.VMEM((n_blk, tok, BLK), F32),
                pltpu.VMEM((n_blk, tok, BLK), F32),
                pltpu.VMEM((tok, d), BF16),
                dma((RING,)), dma((RING,)), dma((2, 4)), dma((4,)),
                dma((3,)), dma((3,)), dma((3,)), dma((3,)),
                dma((n_blk,)), dma((n_blk,)), dma((n_blk,)), dma((n_blk,)), dma((n_blk,)), dma((n_blk,)),
                dma((n_blk,)),
            ],
            compiler_params=pltpu.CompilerParams(
                collective_id=0, has_side_effects=True, vmem_limit_bytes=67043328),
            name="moe_layer",
        )(hidden, expert_ids.T, norm_w.reshape(d // 128, 128), router_w, w_gate, w_up, w_down)

    token_spec = P(("dp", "ep"), None)
    return jax.shard_map(per_device, mesh=mesh, in_specs=(token_spec, token_spec, P(None), P(None, None), P("ep", None, "tp"), P("ep", None, "tp"), P("ep", "tp", None)), out_specs=token_spec, check_vma=False)
```

time: 323 us -> 99 us (0.31)
  waiting for transfers between devices: 146 us -> 0 us
  Pallas kernels: 0 us -> 97.2 us
  matrix products: 59 us -> 0 us
  blocking collectives: 52.7 us -> 0 us
  local copies, waits for them, and re-layouts: 36.5 us -> 1.67 us
  between operations: 13.6 us -> 0.01 us
  other arithmetic: 9.62 us -> 0 us
  starting transfers between devices: 5.21 us -> 0 us
    psum x1 -> x0, waiting for transfers between devices: 103 us -> none  [per_device(): expert_out = lax.psum(part_out, 'tp')]
    pallas_call x0 -> x1, Pallas kernels: none -> 97.2 us  [per_device(): pl.pallas_call(functools.partial(moe_kernel, dims), out_shape=jax.ShapeDt...]
    dot_general x4 -> x0, matrix products: 59 us -> none  [the longest x1 19.7 us: per_device(): jnp.einsum('erf,efd->erd', act_rows, w_down, preferred_element_type=jnp.f...]
    all_to_all x1 -> x0, blocking collectives: 52.7 us -> none  [per_device(): lax.all_to_all(send_rows, 'ep', 0, 2, tiled=True)]
    all_to_all x1 -> x0, waiting for transfers between devices: 42.9 us -> none  [per_device(): lax.all_to_all(expert_out.reshape(1, local_exp, ep_size * row_limit, mode...]
    gather x7 -> x0, local copies, waits for them, and re-layouts: 17.1 us -> none  [the longest x1 7.18 us: per_device(): back_rows.reshape(n_slots, model_dim)[slot_dest]]
    all_to_all x1 -> x0, local copies, waits for them, and re-layouts: 6.51 us -> none  [per_device(): lax.all_to_all(expert_out.reshape(1, local_exp, ep_size * row_limit, mode...]
    psum x1 -> x0, local copies, waits for them, and re-layouts: 6.45 us -> none  [per_device(): expert_out = lax.psum(part_out, 'tp')]
  transfers between devices with their start and end apart: 2 -> 0, of which waited for: 2 -> 0; matrix products, arithmetic and copies ran while one was open for 1% -> 0% of each run, Pallas kernels for 0% -> 0%
where the time goes in v1:
time: 99 us; the launch traced here: 98.9 us
  Pallas kernels  97.2 us (98%)
  local copies, waits for them, and re-layouts  1.67 us (2%)
    pallas_call x1, Pallas kernels, per_device(): pl.pallas_call(functools.partial(moe_kernel, dims), out_shape=jax.ShapeDt...  97.2 us

profile of v1, /device:TPU:0, one launch (start us, length us, event | category | flops | bytes accessed | tf_op | source)
XLA Modules:
  0.0 98.9 jit_solution(4283212087344882404)
XLA Ops:
  0.0 97.2 %moe_layer.1 = bf16[64,2048]{1,0:T(8,128)(2,1)} custom-call(bf16[64,2048]{1,0:T(8,128)(2,1)} %h_hbm.1, s32[8,64]{1,0:T(8,128)} %bitcast.2, bf16[16,128]{1,0:T(8,128)(2,1)} %bitcast.3, bf16[2048,128]{1,0:T(8,128)(2,1)} %rw_hbm.1, bf16[32,2048,384]{2,1,0:T(8,128)(2,1)} %wg_hbm.1, bf16[32,2048,384]{2,1,0:T(8,128)(2,1)} %wu_hbm.1, bf16[32,384,2048]{2,1,0:T(8,128)(2,1)} %wd_hbm.1), custom_call_target="tpu_custom_call" | custom-call | tf_op jit(solution)/shard_map/moe_layer/pallas_call | solution.py:296
  97.2 1.7 %copy.9 = bf16[64,2048]{1,0:T(8,128)(2,1)} copy(bf16[64,2048]{1,0:T(8,128)(2,1)} %moe_layer.1) | data formatting | bytes 524288

commit v2 on v1

--- a/solution.py
+++ b/solution.py
@@ -9,6 +9,8 @@
 
 NORM_EPS = 1e-6
 RING = 10
+UP_UNROLL = 2
+DOWN_UNROLL = 8
 BLK = 256
 F32 = jnp.float32
 BF16 = jnp.bfloat16
@@ -146,22 +148,26 @@
 
     lax.fori_loop(0, d // 256, gather_cols, 0)
 
-    def gate_up(e, carry):
-        slot = lax.rem(e, RING)
-        rows = pl.ds(pl.multiple_of(e * slot_rows, slot_rows), slot_rows)
-        for cp in w_copies(e, slot):
-            cp.wait()
-        pre = jnp.dot(xbuf[rows, :], ring[slot], preferred_element_type=F32)
-        gate, up = pre[:, :ff], pre[:, ff:]
-        abuf[rows, :] = (gate * jax.nn.sigmoid(gate) * up).astype(BF16)
-
-        @pl.when(e + RING < local)
-        def _():
-            for cp in w_copies(e + RING, slot):
-                cp.start()
+    def gate_up(i, carry):
+        first = i * UP_UNROLL
+        for u in range(UP_UNROLL):
+            for cp in w_copies(first + u, lax.rem(first + u, RING)):
+                cp.wait()
+        for u in range(UP_UNROLL):
+            e = first + u
+            rows = pl.ds(pl.multiple_of(e * slot_rows, slot_rows), slot_rows)
+            pre = jnp.dot(xbuf[rows, :], ring[lax.rem(e, RING)], preferred_element_type=F32)
+            gate, up = pre[:, :ff], pre[:, ff:]
+            abuf[rows, :] = (gate * jax.nn.sigmoid(gate) * up).astype(BF16)
+
+        @pl.when(first + RING < local)
+        def _():
+            for u in range(UP_UNROLL):
+                for cp in w_copies(first + u + RING, lax.rem(first + u, RING)):
+                    cp.start()
         return carry
 
-    lax.fori_loop(0, local, gate_up, 0)
+    lax.fori_loop(0, local // UP_UNROLL, gate_up, 0)
 
     rw_c.wait()
     logits = jnp.dot(vbuf[...], rwb[...], preferred_element_type=F32)
@@ -226,13 +232,15 @@
         for k in range(parts):
             d_copy(c, s, k).wait()
 
-        def one(e, inner):
-            rows = pl.ds(pl.multiple_of(e * slot_rows, slot_rows), slot_rows)
-            y = jnp.dot(abuf[rows, :], wdb[s, e], preferred_element_type=F32)
-            ybuf[rows, :] = y.astype(BF16)
+        def some(i, inner):
+            for u in range(DOWN_UNROLL):
+                e = i * DOWN_UNROLL + u
+                rows = pl.ds(pl.multiple_of(e * slot_rows, slot_rows), slot_rows)
+                y = jnp.dot(abuf[rows, :], wdb[s, e], preferred_element_type=F32)
+                ybuf[rows, :] = y.astype(BF16)
             return inner
 
-        lax.fori_loop(0, local, one, 0)
+        lax.fori_loop(0, local // DOWN_UNROLL, some, 0)
 
         @pl.when(c + 2 < n_blk)
         def _():

time: 99 us -> 72.8 us (0.74)
  Pallas kernels: 97.2 us -> 71 us
    pallas_call x1, Pallas kernels: 97.2 us -> 71 us  [per_device(): pl.pallas_call(functools.partial(moe_kernel, dims), out_shape=jax.ShapeDt...]
where the time goes in v2:
time: 72.8 us; the launch traced here: 72.7 us
  Pallas kernels  71 us (98%)
  local copies, waits for them, and re-layouts  1.67 us (2%)
    pallas_call x1, Pallas kernels, per_device(): pl.pallas_call(functools.partial(moe_kernel, dims), out_shape=jax.ShapeDt...  71 us
    unnamed x1, local copies, waits for them, and re-layouts  1.67 us

profile of v2, /device:TPU:0, one launch (start us, length us, event | category | flops | bytes accessed | tf_op | source)
XLA Modules:
  0.0 72.7 jit_solution(10749753790116628949)
XLA Ops:
  0.0 71.0 %moe_layer.1 = bf16[64,2048]{1,0:T(8,128)(2,1)} custom-call(bf16[64,2048]{1,0:T(8,128)(2,1)} %h_hbm.1, s32[8,64]{1,0:T(8,128)} %bitcast.2, bf16[16,128]{1,0:T(8,128)(2,1)} %bitcast.3, bf16[2048,128]{1,0:T(8,128)(2,1)} %rw_hbm.1, bf16[32,2048,384]{2,1,0:T(8,128)(2,1)} %wg_hbm.1, bf16[32,2048,384]{2,1,0:T(8,128)(2,1)} %wu_hbm.1, bf16[32,384,2048]{2,1,0:T(8,128)(2,1)} %wd_hbm.1), custom_call_target="tpu_custom_call" | custom-call | tf_op jit(solution)/shard_map/moe_layer/pallas_call | solution.py:304
  71.0 1.7 %copy.9 = bf16[64,2048]{1,0:T(8,128)(2,1)} copy(bf16[64,2048]{1,0:T(8,128)(2,1)} %moe_layer.1) | data formatting | bytes 524288

commit v3 on v2

v3 whole, which is shorter than its diff:
```python
import functools

import jax
import jax.numpy as jnp
from jax import lax
from jax.experimental import pallas as pl
from jax.experimental.pallas import tpu as pltpu
from jax.sharding import PartitionSpec as P

NORM_EPS = 1e-6
POOL = 15
BLK = 256
UP_UNROLL = 2
LAG_B, LAG_C, LAG_D = 1, 3, 6
F32 = jnp.float32
BF16 = jnp.bfloat16


def row_cap(tok_dev, top_k, n_experts):
    return 8 * ((2 * top_k * tok_dev + 8 * n_experts - 1) // (8 * n_experts))


def moe_kernel(dims, h_hbm, ids_hbm, nw_hbm, rw_hbm, wg_hbm, wu_hbm, wd_hbm, out_hbm,
               pool, hbuf, idb, nwb, rwb, vbuf, xbuf, posb, cbuf, abuf, ybuf,
               sbuf, ra, tb, rb, zb, rc, obuf,
               wsem, lsem, hs_sem, hr_sem, is_sem, ir_sem,
               as_sem, ar_sem, bs_sem, br_sem, cs_sem, cr_sem, osem):
    tok, top_k, n_exp, local, ff, d, cap = dims
    n_tok = 4 * tok
    chip_tok = 2 * tok
    chip_rows = 2 * cap
    slot_rows = 4 * cap
    n_slots = local * slot_rows
    n_blk = d // BLK
    groups = 2 * ff // BLK
    per = groups * d // ff
    n_half = local // per
    n_chunks = local + n_blk * n_half
    ep = lax.axis_index("ep")
    x = ep // 2
    core = ep % 2
    partner = {"ep": x * 2 + (1 - core)}
    across = {"ep": (1 - x) * 2 + core}
    other = {"tp": 1 - lax.axis_index("tp")}
    MESH = pl.DeviceIdType.MESH
    q_own, q_partner = core, 1 - core
    q_across, q_diag = 2 + core, 3 - core

    def up_copies(e, slot):
        return [
            pltpu.make_async_copy(src.at[e], pool.at[slot, :, pl.ds(k * ff, ff)], wsem.at[slot, k])
            for k, src in enumerate((wg_hbm, wu_hbm))]

    def down_copies(j, slot):
        cols = pl.ds(pl.multiple_of((j // n_half) * BLK, BLK), BLK)
        first = (j % n_half) * per * ff
        return [
            pltpu.make_async_copy(
                wd_hbm.at[pl.ds(pl.multiple_of(first + g * d, d), d), cols],
                pool.at[slot, :, pl.ds(g * BLK, BLK)], wsem.at[slot, g])
            for g in range(groups)]

    def start_chunk(i):
        slot = lax.rem(i, POOL)

        @pl.when(i < local)
        def _():
            for cp in up_copies(i, slot):
                cp.start()

        @pl.when((i >= local) & (i < n_chunks))
        def _():
            for cp in down_copies(i - local, slot):
                cp.start()

    own_h = pltpu.make_async_copy(h_hbm, hbuf.at[q_own], lsem.at[0])
    own_i = pltpu.make_async_copy(ids_hbm, idb.at[q_own], lsem.at[1])
    nw_c = pltpu.make_async_copy(nw_hbm, nwb, lsem.at[2])
    rw_c = pltpu.make_async_copy(rw_hbm, rwb, lsem.at[3])
    own_h.start()
    own_i.start()
    nw_c.start()

    barrier = pltpu.get_barrier_semaphore()
    for dev in (partner, across, other):
        pl.semaphore_signal(barrier, inc=1, device_id=dev, device_id_type=MESH)

    def first_chunk(i, carry):
        for cp in up_copies(i, i):
            cp.start()
        return carry

    lax.fori_loop(0, POOL, first_chunk, 0)
    rw_c.start()
    own_h.wait()
    own_i.wait()
    pl.semaphore_wait(barrier, 3)

    def h_copy(q, dst, dev, n):
        return pltpu.make_async_remote_copy(
            src_ref=hbuf.at[q], dst_ref=hbuf.at[dst], send_sem=hs_sem.at[n], recv_sem=hr_sem.at[n],
            device_id=dev, device_id_type=MESH)

    def i_copy(q, dst, dev, n):
        return pltpu.make_async_remote_copy(
            src_ref=idb.at[q], dst_ref=idb.at[dst], send_sem=is_sem.at[n], recv_sem=ir_sem.at[n],
            device_id=dev, device_id_type=MESH)

    i_x = i_copy(q_own, q_across, across, 0)
    i_p = i_copy(q_own, q_own, partner, 1)
    i_r = i_copy(q_across, q_across, partner, 2)
    h_x = h_copy(q_own, q_across, across, 0)
    h_p = h_copy(q_own, q_own, partner, 1)
    h_r = h_copy(q_across, q_across, partner, 2)
    i_x.start()
    h_x.start()
    i_p.start()
    h_p.start()

    nw_c.wait()

    def norm_rows(q):
        wide = hbuf[q].astype(F32)
        inv = lax.rsqrt(jnp.mean(wide * wide, axis=-1, keepdims=True) + NORM_EPS)
        for k in range(d // 128):
            cols = pl.ds(k * 128, 128)
            part = hbuf[q, :, cols].astype(F32) * inv * nwb[k:k + 1, :].astype(F32)
            vbuf[pl.ds(pl.multiple_of(q * tok, tok), tok), cols] = part.astype(BF16)

    norm_rows(q_own)
    i_copy(q_partner, q_partner, partner, 1).wait_recv()
    i_x.wait_recv()
    i_r.start()
    i_copy(q_diag, q_diag, partner, 2).wait_recv()

    ids_t = jnp.concatenate([idb[q] for q in range(4)], axis=1)
    exp_iota = lax.broadcasted_iota(jnp.int32, (n_exp, n_tok), 0)
    member = jnp.zeros((n_exp, n_tok), F32)
    for j in range(top_k):
        member = member + jnp.where(ids_t[j:j + 1, :] == exp_iota, 1.0, 0.0)
    row_i = lax.broadcasted_iota(jnp.int32, (n_tok, n_tok), 0)
    col_i = lax.broadcasted_iota(jnp.int32, (n_tok, n_tok), 1)
    before = (row_i < col_i) & (row_i // chip_tok == col_i // chip_tok)
    pos = jnp.dot(member.astype(BF16), jnp.where(before, 1.0, 0.0).astype(BF16), preferred_element_type=F32)
    posb[...] = jnp.where(member > 0.5, pos, -1.0)

    h_copy(q_partner, q_partner, partner, 1).wait_recv()
    norm_rows(q_partner)

    pos_loc = posb[pl.ds(pl.multiple_of(ep * local, local), local), :]
    rank_f = lax.broadcasted_iota(jnp.int32, (chip_rows, chip_tok), 0).astype(F32)

    def gather_rows(chip):
        pos_chip = pos_loc[:, chip * chip_tok:(chip + 1) * chip_tok]
        pick = jnp.concatenate(
            [jnp.where(pos_chip[e:e + 1, :] == rank_f, 1.0, 0.0).astype(BF16) for e in range(local)], axis=0)

        def cols_step(n, carry):
            cols = pl.ds(pl.multiple_of(n * 256, 256), 256)
            v_cols = vbuf[chip * chip_tok:(chip + 1) * chip_tok, cols]
            rows = jnp.dot(pick, v_cols, preferred_element_type=F32).astype(BF16)
            xbuf[:, chip, :, cols] = rows.reshape(local, chip_rows, 256)
            return carry

        lax.fori_loop(0, d // 256, cols_step, 0)

    gather_rows(0)
    h_x.wait_recv()
    h_r.start()
    norm_rows(q_across)
    h_copy(q_diag, q_diag, partner, 2).wait_recv()
    norm_rows(q_diag)
    gather_rows(1)

    def gate_up(i, carry):
        first = i * UP_UNROLL
        for u in range(UP_UNROLL):
            for cp in up_copies(first + u, lax.rem(first + u, POOL)):
                cp.wait()
        for u in range(UP_UNROLL):
            e = first + u
            rows = pl.ds(pl.multiple_of(e * slot_rows, slot_rows), slot_rows)
            pre = jnp.dot(xbuf[e].reshape(slot_rows, d), pool[lax.rem(e, POOL)], preferred_element_type=F32)
            gate, up = pre[:, :ff], pre[:, ff:]
            abuf[rows, :] = (gate * jax.nn.sigmoid(gate) * up).astype(BF16)
        for u in range(UP_UNROLL):
            start_chunk(first + u + POOL)
        return carry

    trips = local // UP_UNROLL
    lax.fori_loop(0, trips // 2, gate_up, 0)

    rw_c.wait()
    logits = jnp.dot(vbuf[...], rwb[...], preferred_element_type=F32)
    expo = jnp.exp(logits - jnp.max(logits, axis=-1, keepdims=True))
    prob = expo / jnp.sum(expo, axis=-1, keepdims=True)
    g_hi = prob.astype(BF16)
    rest = prob - g_hi.astype(F32)
    g_mid = rest.astype(BF16)
    g_lo = (rest - g_mid.astype(F32)).astype(BF16)
    chip_of = lax.broadcasted_iota(jnp.int32, (n_exp, n_tok), 1) // chip_tok
    pos_all = posb[...]
    pos_all = jnp.where(pos_all < 0.0, -1.0, pos_all + (chip_of * chip_rows).astype(F32))
    pos_t = pos_all.T.astype(BF16)
    for n in range(n_slots // 256):
        lane = lax.broadcasted_iota(jnp.int32, (n_exp, 256), 1) + n * 256
        sub = lax.broadcasted_iota(jnp.int32, (n_exp, 256), 0)
        spread = jnp.where(sub == ep * local + lane // slot_rows, 1.0, 0.0).astype(BF16)
        want = (lax.broadcasted_iota(jnp.int32, (n_tok, 256), 1) % slot_rows).astype(F32)
        hit = jnp.dot(pos_t, spread, preferred_element_type=F32) == want
        for i, g in enumerate((g_hi, g_mid, g_lo)):
            wide_g = jnp.dot(g, spread, preferred_element_type=F32)
            cbuf[i, :, n * 256:(n + 1) * 256] = jnp.where(hit, wide_g, 0.0).astype(BF16)

    lax.fori_loop(trips // 2, trips, gate_up, 0)

    def a_copy(c):
        return pltpu.make_async_remote_copy(
            src_ref=sbuf.at[c, :, 1 - core], dst_ref=ra.at[c],
            send_sem=as_sem.at[c], recv_sem=ar_sem.at[c], device_id=partner, device_id_type=MESH)

    def b_copy(c):
        return pltpu.make_async_remote_copy(
            src_ref=tb.at[c, 1], dst_ref=rb.at[c],
            send_sem=bs_sem.at[c], recv_sem=br_sem.at[c], device_id=across, device_id_type=MESH)

    def c_copy(c):
        return pltpu.make_async_remote_copy(
            src_ref=zb.at[c], dst_ref=rc.at[c],
            send_sem=cs_sem.at[c], recv_sem=cr_sem.at[c], device_id=other, device_id_type=MESH)

    def o_copy(c):
        cols = pl.ds(pl.multiple_of(c * BLK, BLK), BLK)
        return pltpu.make_async_copy(obuf.at[:, cols], out_hbm.at[:, cols], osem.at[c])

    def stage_b(c):
        a_copy(c).wait_recv()
        tb[c] = sbuf[c, :, core] + ra[c]
        b_copy(c).start()

    def stage_c(c):
        b_copy(c).wait_recv()
        zb[c] = tb[c, 0] + rb[c]
        c_copy(c).start()

    def stage_d(c):
        c_copy(c).wait_recv()
        cols = pl.ds(pl.multiple_of(c * BLK, BLK), BLK)
        obuf[:, cols] = (hbuf[q_own, :, cols].astype(F32) + (zb[c] + rc[c])).astype(BF16)
        o_copy(c).start()

    def down(c, carry):
        for h in range(n_half):
            j = c * n_half + h
            slot = lax.rem(local + j, POOL)
            for cp in down_copies(j, slot):
                cp.wait()
            for k in range(per):
                e = h * per + k
                act = abuf[e * slot_rows:(e + 1) * slot_rows, :]
                first, last = k * ff, (k + 1) * ff
                y = None
                while first < last:
                    g, row = first // d, first % d
                    size = min(last - first, d - row)
                    lo = first - k * ff
                    part = jnp.dot(act[:, lo:lo + size], pool[slot, row:row + size, g * BLK:(g + 1) * BLK],
                                   preferred_element_type=F32)
                    y = part if y is None else y + part
                    first += size
                ybuf[k * slot_rows:(k + 1) * slot_rows, :] = y.astype(BF16)
            start_chunk(local + j + POOL)
            y_all = ybuf[...]
            slots = pl.ds(h * per * slot_rows, per * slot_rows)
            total = jnp.dot(cbuf[2, :, slots], y_all, preferred_element_type=F32)
            total = total + jnp.dot(cbuf[1, :, slots], y_all, preferred_element_type=F32)
            total = total + jnp.dot(cbuf[0, :, slots], y_all, preferred_element_type=F32)
            total = total.reshape(2, 2, tok, BLK)
            if h == 0:
                sbuf[c] = total
            else:
                sbuf[c] += total
        a_copy(c).start()

        for lag, stage in ((LAG_B, stage_b), (LAG_C, stage_c), (LAG_D, stage_d)):
            @pl.when(c >= lag)
            def _(lag=lag, stage=stage):
                stage(c - lag)
        return carry

    lax.fori_loop(0, n_blk, down, 0)
    for step in range(n_blk, n_blk + LAG_D):
        for lag, stage in ((LAG_B, stage_b), (LAG_C, stage_c), (LAG_D, stage_d)):
            if step - lag < n_blk:
                stage(step - lag)

    for cp in (i_x, i_p, i_r, h_x, h_p, h_r):
        cp.wait_send()

    def drain(c, carry):
        a_copy(c).wait_send()
        b_copy(c).wait_send()
        c_copy(c).wait_send()
        o_copy(c).wait()
        return carry

    lax.fori_loop(0, n_blk, drain, 0)


def solution(mesh):
    def per_device(hidden, expert_ids, norm_w, router_w, w_gate, w_up, w_down):
        tok, d = hidden.shape
        top_k = expert_ids.shape[1]
        n_exp = router_w.shape[1]
        local, _, ff = w_gate.shape
        cap = row_cap(tok, top_k, n_exp)
        dims = (tok, top_k, n_exp, local, ff, d, cap)
        n_tok = 4 * tok
        n_slots = local * 4 * cap
        n_blk = d // BLK
        groups = 2 * ff // BLK
        any_spec = pl.BlockSpec(memory_space=pl.ANY)
        dma = pltpu.SemaphoreType.DMA
        return pl.pallas_call(
            functools.partial(moe_kernel, dims),
            out_shape=jax.ShapeDtypeStruct((tok, d), BF16),
            in_specs=[any_spec] * 7,
            out_specs=any_spec,
            scratch_shapes=[
                pltpu.VMEM((POOL, d, 2 * ff), BF16),
                pltpu.VMEM((4, tok, d), BF16),
                pltpu.VMEM((4, top_k, tok), jnp.int32),
                pltpu.VMEM((d // 128, 128), BF16),
                pltpu.VMEM((d, n_exp), BF16),
                pltpu.VMEM((n_tok, d), BF16),
                pltpu.VMEM((local, 2, 2 * cap, d), BF16),
                pltpu.VMEM((n_exp, n_tok), F32),
                pltpu.VMEM((3, n_tok, n_slots), BF16),
                pltpu.VMEM((n_slots, ff), BF16),
                pltpu.VMEM((groups * d // ff * 4 * cap, BLK), BF16),
                pltpu.VMEM((n_blk, 2, 2, tok, BLK), F32),
                pltpu.VMEM((n_blk, 2, tok, BLK), F32),
                pltpu.VMEM((n_blk, 2, tok, BLK), F32),
                pltpu.VMEM((n_blk, tok, BLK), F32),
                pltpu.VMEM((n_blk, tok, BLK), F32),
                pltpu.VMEM((n_blk, tok, BLK), F32),
                pltpu.VMEM((tok, d), BF16),
                dma((POOL, groups)), dma((4,)),
                dma((3,)), dma((3,)), dma((3,)), dma((3,)),
                dma((n_blk,)), dma((n_blk,)), dma((n_blk,)), dma((n_blk,)), dma((n_blk,)), dma((n_blk,)),
                dma((n_blk,)),
            ],
            compiler_params=pltpu.CompilerParams(
                collective_id=0, has_side_effects=True, vmem_limit_bytes=67043328),
            name="moe_layer",
        )(hidden, expert_ids.T, norm_w.reshape(d // 128, 128), router_w, w_gate, w_up, w_down.reshape(local * ff, d))

    token_spec = P(("dp", "ep"), None)
    return jax.shard_map(per_device, mesh=mesh, in_specs=(token_spec, token_spec, P(None), P(None, None), P("ep", None, "tp"), P("ep", None, "tp"), P("ep", "tp", None)), out_specs=token_spec, check_vma=False)
```

time: 72.8 us -> 63.2 us (0.87)
  Pallas kernels: 71 us -> 61.4 us
    pallas_call x1, Pallas kernels: 71 us -> 61.4 us  [per_device(): pl.pallas_call(functools.partial(moe_kernel, dims), out_shape=jax.ShapeDt...]
where the time goes in v3:
time: 63.2 us; the launch traced here: 63.1 us
  Pallas kernels  61.4 us (97%)
  local copies, waits for them, and re-layouts  1.67 us (3%)
    pallas_call x1, Pallas kernels, per_device(): pl.pallas_call(functools.partial(moe_kernel, dims), out_shape=jax.ShapeDt...  61.4 us
    unnamed x1, local copies, waits for them, and re-layouts  1.67 us

profile of v3, /device:TPU:0, one launch (start us, length us, event | category | flops | bytes accessed | tf_op | source)
XLA Modules:
  0.0 63.1 jit_solution(12983898049098215624)
XLA Ops:
  0.0 61.4 %moe_layer.1 = bf16[64,2048]{1,0:T(8,128)(2,1)} custom-call(bf16[64,2048]{1,0:T(8,128)(2,1)} %h_hbm.1, s32[8,64]{1,0:T(8,128)} %bitcast.4, bf16[16,128]{1,0:T(8,128)(2,1)} %bitcast.5, bf16[2048,128]{1,0:T(8,128)(2,1)} %rw_hbm.1, bf16[32,2048,384]{2,1,0:T(8,128)(2,1)} %wg_hbm.1, bf16[32,2048,384]{2,1,0:T(8,128)(2,1)} %wu_hbm.1, bf16[12288,2048]{1,0:T(8,128)(2,1)} %bitcast.3), custom_call_target="tpu_custom_call" | custom-call | tf_op jit(solution)/shard_map/moe_layer/pallas_call | solution.py:324
  61.4 1.7 %copy.9 = bf16[64,2048]{1,0:T(8,128)(2,1)} copy(bf16[64,2048]{1,0:T(8,128)(2,1)} %moe_layer.1) | data formatting | bytes 524288

commit v4 on v3

--- a/solution.py
+++ b/solution.py
@@ -10,8 +10,8 @@
 NORM_EPS = 1e-6
 POOL = 15
 BLK = 256
+LAST = 128
 UP_UNROLL = 2
-LAG_B, LAG_C, LAG_D = 1, 3, 6
 F32 = jnp.float32
 BF16 = jnp.bfloat16
 
@@ -20,28 +20,31 @@
     return 8 * ((2 * top_k * tok_dev + 8 * n_experts - 1) // (8 * n_experts))
 
 
-def moe_kernel(dims, h_hbm, ids_hbm, nw_hbm, rw_hbm, wg_hbm, wu_hbm, wd_hbm, out_hbm,
+def moe_kernel(dims, h_hbm, ids_hbm, nw_hbm, rw_hbm, wg_hbm, wu_hbm, wd_hbm, out_ref,
                pool, hbuf, idb, nwb, rwb, vbuf, xbuf, posb, cbuf, abuf, ybuf,
-               sbuf, ra, tb, rb, zb, rc, obuf,
+               sbuf, ra, tb, rb, zb, rc, ylast, slast, ra2, tb2, r2,
                wsem, lsem, hs_sem, hr_sem, is_sem, ir_sem,
-               as_sem, ar_sem, bs_sem, br_sem, cs_sem, cr_sem, osem):
+               as_sem, ar_sem, bs_sem, br_sem, cs_sem, cr_sem,
+               as2_sem, ar2_sem, xs2_sem, xr2_sem):
     tok, top_k, n_exp, local, ff, d, cap = dims
     n_tok = 4 * tok
     chip_tok = 2 * tok
     chip_rows = 2 * cap
     slot_rows = 4 * cap
     n_slots = local * slot_rows
-    n_blk = d // BLK
+    n_big = d // BLK - 1
     groups = 2 * ff // BLK
     per = groups * d // ff
     n_half = local // per
-    n_chunks = local + n_blk * n_half
+    n_wide = local + n_big * n_half
+    n_chunks = n_wide + BLK // LAST
     ep = lax.axis_index("ep")
     x = ep // 2
     core = ep % 2
     partner = {"ep": x * 2 + (1 - core)}
     across = {"ep": (1 - x) * 2 + core}
     other = {"tp": 1 - lax.axis_index("tp")}
+    diag = {**other, **across}
     MESH = pl.DeviceIdType.MESH
     q_own, q_partner = core, 1 - core
     q_across, q_diag = 2 + core, 3 - core
@@ -60,6 +63,14 @@
                 pool.at[slot, :, pl.ds(g * BLK, BLK)], wsem.at[slot, g])
             for g in range(groups)]
 
+    def last_copies(f, slot):
+        cols = pl.ds(pl.multiple_of(n_big * BLK + f * LAST, LAST), LAST)
+        return [
+            pltpu.make_async_copy(
+                wd_hbm.at[pl.ds(h * per * ff + g * d, d), cols],
+                pool.at[slot, :, pl.ds(g * BLK + h * LAST, LAST)], wsem.at[slot, h * groups + g])
+            for h in range(n_half) for g in range(groups)]
+
     def start_chunk(i):
         slot = lax.rem(i, POOL)
 
@@ -68,9 +79,14 @@
             for cp in up_copies(i, slot):
                 cp.start()
 
-        @pl.when((i >= local) & (i < n_chunks))
+        @pl.when((i >= local) & (i < n_wide))
         def _():
             for cp in down_copies(i - local, slot):
+                cp.start()
+
+        @pl.when((i >= n_wide) & (i < n_chunks))
+        def _():
+            for cp in last_copies(i - n_wide, slot):
                 cp.start()
 
     own_h = pltpu.make_async_copy(h_hbm, hbuf.at[q_own], lsem.at[0])
@@ -82,7 +98,7 @@
     nw_c.start()
 
     barrier = pltpu.get_barrier_semaphore()
-    for dev in (partner, across, other):
+    for dev in (partner, across, other, diag):
         pl.semaphore_signal(barrier, inc=1, device_id=dev, device_id_type=MESH)
 
     def first_chunk(i, carry):
@@ -94,7 +110,7 @@
     rw_c.start()
     own_h.wait()
     own_i.wait()
-    pl.semaphore_wait(barrier, 3)
+    pl.semaphore_wait(barrier, 4)
 
     def h_copy(q, dst, dev, n):
         return pltpu.make_async_remote_copy(
@@ -216,7 +232,7 @@
 
     def a_copy(c):
         return pltpu.make_async_remote_copy(
-            src_ref=sbuf.at[c, :, 1 - core], dst_ref=ra.at[c],
+            src_ref=sbuf.at[c + 1, :, 1 - core], dst_ref=ra.at[c],
             send_sem=as_sem.at[c], recv_sem=ar_sem.at[c], device_id=partner, device_id_type=MESH)
 
     def b_copy(c):
@@ -229,13 +245,9 @@
             src_ref=zb.at[c], dst_ref=rc.at[c],
             send_sem=cs_sem.at[c], recv_sem=cr_sem.at[c], device_id=other, device_id_type=MESH)
 
-    def o_copy(c):
-        cols = pl.ds(pl.multiple_of(c * BLK, BLK), BLK)
-        return pltpu.make_async_copy(obuf.at[:, cols], out_hbm.at[:, cols], osem.at[c])
-
     def stage_b(c):
         a_copy(c).wait_recv()
-        tb[c] = sbuf[c, :, core] + ra[c]
+        tb[c] = sbuf[c + 1, :, core] + ra[c]
         b_copy(c).start()
 
     def stage_c(c):
@@ -246,53 +258,137 @@
     def stage_d(c):
         c_copy(c).wait_recv()
         cols = pl.ds(pl.multiple_of(c * BLK, BLK), BLK)
-        obuf[:, cols] = (hbuf[q_own, :, cols].astype(F32) + (zb[c] + rc[c])).astype(BF16)
-        o_copy(c).start()
+        out_ref[:, cols] = (hbuf[q_own, :, cols].astype(F32) + (zb[c] + rc[c])).astype(BF16)
+
+    def a2_copy(f):
+        return pltpu.make_async_remote_copy(
+            src_ref=slast.at[f, :, 1 - core], dst_ref=ra2.at[f],
+            send_sem=as2_sem.at[f], recv_sem=ar2_sem.at[f], device_id=partner, device_id_type=MESH)
+
+    def x2_copies(f):
+        return [
+            pltpu.make_async_remote_copy(
+                src_ref=tb2.at[f, src], dst_ref=r2.at[f, n],
+                send_sem=xs2_sem.at[f, n], recv_sem=xr2_sem.at[f, n], device_id=dev, device_id_type=MESH)
+            for n, (src, dev) in enumerate(((1, diag), (1, across), (0, other)))]
+
+    def stage_x2(f):
+        a2_copy(f).wait_recv()
+        tb2[f] = slast[f, :, core] + ra2[f]
+        for cp in x2_copies(f):
+            cp.start()
+
+    def stage_d2(f):
+        for cp in x2_copies(f):
+            cp.wait_recv()
+        cols = pl.ds(n_big * BLK + f * LAST, LAST)
+        moe = (tb2[f, 0] + r2[f, 1]) + (r2[f, 2] + r2[f, 0])
+        out_ref[:, cols] = (hbuf[q_own, :, cols].astype(F32) + moe).astype(BF16)
+
+    def act_rows(e):
+        return abuf[e * slot_rows:(e + 1) * slot_rows, :]
+
+    def split_k(k):
+        first, last = k * ff, (k + 1) * ff
+        while first < last:
+            g, row = first // d, first % d
+            size = min(last - first, d - row)
+            yield g, row, size, first - k * ff
+            first += size
+
+    def down_half(slot, h):
+        for k in range(per):
+            act = act_rows(h * per + k)
+            y = None
+            for g, row, size, lo in split_k(k):
+                part = jnp.dot(act[:, lo:lo + size], pool[slot, row:row + size, g * BLK:(g + 1) * BLK],
+                               preferred_element_type=F32)
+                y = part if y is None else y + part
+            ybuf[h, k * slot_rows:(k + 1) * slot_rows, :] = y.astype(BF16)
+
+    def down_last(slot):
+        for k in range(per):
+            act = jnp.concatenate([act_rows(h * per + k) for h in range(n_half)], axis=0)
+            y = None
+            for g, row, size, lo in split_k(k):
+                part = jnp.dot(act[:, lo:lo + size], pool[slot, row:row + size, g * BLK:(g + 1) * BLK],
+                               preferred_element_type=F32)
+                y = part if y is None else y + part
+            for h in range(n_half):
+                e = h * per + k
+                ylast[e * slot_rows:(e + 1) * slot_rows, :] = (
+                    y[h * slot_rows:(h + 1) * slot_rows, h * LAST:(h + 1) * LAST].astype(BF16))
+
+    def combine(y_all, slots):
+        total = jnp.dot(cbuf[2, :, slots], y_all, preferred_element_type=F32)
+        total = total + jnp.dot(cbuf[1, :, slots], y_all, preferred_element_type=F32)
+        return total + jnp.dot(cbuf[0, :, slots], y_all, preferred_element_type=F32)
+
+    half_slots = per * slot_rows
+
+    def combine_half(h):
+        return combine(ybuf[h], pl.ds(h * half_slots, half_slots)).reshape(2, 2, tok, BLK)
+
+    def wait_down(j):
+        slot = lax.rem(local + j, POOL)
+        for cp in down_copies(j, slot):
+            cp.wait()
+        return slot
 
     def down(c, carry):
-        for h in range(n_half):
-            j = c * n_half + h
-            slot = lax.rem(local + j, POOL)
-            for cp in down_copies(j, slot):
-                cp.wait()
-            for k in range(per):
-                e = h * per + k
-                act = abuf[e * slot_rows:(e + 1) * slot_rows, :]
-                first, last = k * ff, (k + 1) * ff
-                y = None
-                while first < last:
-                    g, row = first // d, first % d
-                    size = min(last - first, d - row)
-                    lo = first - k * ff
-                    part = jnp.dot(act[:, lo:lo + size], pool[slot, row:row + size, g * BLK:(g + 1) * BLK],
-                                   preferred_element_type=F32)
-                    y = part if y is None else y + part
-                    first += size
-                ybuf[k * slot_rows:(k + 1) * slot_rows, :] = y.astype(BF16)
-            start_chunk(local + j + POOL)
-            y_all = ybuf[...]
-            slots = pl.ds(h * per * slot_rows, per * slot_rows)
-            total = jnp.dot(cbuf[2, :, slots], y_all, preferred_element_type=F32)
-            total = total + jnp.dot(cbuf[1, :, slots], y_all, preferred_element_type=F32)
-            total = total + jnp.dot(cbuf[0, :, slots], y_all, preferred_element_type=F32)
-            total = total.reshape(2, 2, tok, BLK)
-            if h == 0:
-                sbuf[c] = total
-            else:
-                sbuf[c] += total
-        a_copy(c).start()
-
-        for lag, stage in ((LAG_B, stage_b), (LAG_C, stage_c), (LAG_D, stage_d)):
+        slot = wait_down(2 * c)
+        down_half(slot, 0)
+        sbuf[c] += combine_half(1)
+        start_chunk(local + 2 * c + POOL)
+
+        @pl.when(c >= 1)
+        def _():
+            a_copy(c - 1).start()
+
+        for lag, stage in ((2, stage_b), (4, stage_c), (6, stage_d)):
             @pl.when(c >= lag)
             def _(lag=lag, stage=stage):
                 stage(c - lag)
+
+        slot = wait_down(2 * c + 1)
+        down_half(slot, 1)
+        sbuf[c + 1] = combine_half(0)
+        start_chunk(local + 2 * c + 1 + POOL)
         return carry
 
-    lax.fori_loop(0, n_blk, down, 0)
-    for step in range(n_blk, n_blk + LAG_D):
-        for lag, stage in ((LAG_B, stage_b), (LAG_C, stage_c), (LAG_D, stage_d)):
-            if step - lag < n_blk:
-                stage(step - lag)
+    lax.fori_loop(0, n_big, down, 0)
+
+    all_slots = pl.ds(0, n_slots)
+    slot = (n_chunks - 2) % POOL
+    for cp in last_copies(0, slot):
+        cp.wait()
+    down_last(slot)
+    sbuf[n_big] += combine_half(1)
+    a_copy(n_big - 1).start()
+    stage_b(n_big - 2)
+    stage_c(n_big - 4)
+    slast[0] = combine(ylast[...], all_slots).reshape(2, 2, tok, LAST)
+    a2_copy(0).start()
+    slot = (n_chunks - 1) % POOL
+    for cp in last_copies(1, slot):
+        cp.wait()
+    down_last(slot)
+    slast[1] = combine(ylast[...], all_slots).reshape(2, 2, tok, LAST)
+    a2_copy(1).start()
+    stage_b(n_big - 1)
+    stage_c(n_big - 3)
+    stage_x2(0)
+    stage_x2(1)
+    stage_d(n_big - 6)
+    stage_c(n_big - 2)
+    stage_d(n_big - 5)
+    stage_d(n_big - 4)
+    stage_c(n_big - 1)
+    stage_d(n_big - 3)
+    stage_d2(0)
+    stage_d(n_big - 2)
+    stage_d2(1)
+    stage_d(n_big - 1)
 
     for cp in (i_x, i_p, i_r, h_x, h_p, h_r):
         cp.wait_send()
@@ -301,10 +397,13 @@
         a_copy(c).wait_send()
         b_copy(c).wait_send()
         c_copy(c).wait_send()
-        o_copy(c).wait()
         return carry
 
-    lax.fori_loop(0, n_blk, drain, 0)
+    lax.fori_loop(0, n_big, drain, 0)
+    for f in range(2):
+        a2_copy(f).wait_send()
+        for cp in x2_copies(f):
+            cp.wait_send()
 
 
 def solution(mesh):
@@ -317,15 +416,15 @@
         dims = (tok, top_k, n_exp, local, ff, d, cap)
         n_tok = 4 * tok
         n_slots = local * 4 * cap
-        n_blk = d // BLK
+        n_big = d // BLK - 1
         groups = 2 * ff // BLK
         any_spec = pl.BlockSpec(memory_space=pl.ANY)
         dma = pltpu.SemaphoreType.DMA
         return pl.pallas_call(
             functools.partial(moe_kernel, dims),
-            out_shape=jax.ShapeDtypeStruct((tok, d), BF16),
+            out_shape=pltpu.VMEM((tok, d), BF16),
             in_specs=[any_spec] * 7,
-            out_specs=any_spec,
+            out_specs=pl.BlockSpec(memory_space=pltpu.VMEM),
             scratch_shapes=[
                 pltpu.VMEM((POOL, d, 2 * ff), BF16),
                 pltpu.VMEM((4, tok, d), BF16),
@@ -337,21 +436,25 @@
                 pltpu.VMEM((n_exp, n_tok), F32),
                 pltpu.VMEM((3, n_tok, n_slots), BF16),
                 pltpu.VMEM((n_slots, ff), BF16),
-                pltpu.VMEM((groups * d // ff * 4 * cap, BLK), BF16),
-                pltpu.VMEM((n_blk, 2, 2, tok, BLK), F32),
-                pltpu.VMEM((n_blk, 2, tok, BLK), F32),
-                pltpu.VMEM((n_blk, 2, tok, BLK), F32),
-                pltpu.VMEM((n_blk, tok, BLK), F32),
-                pltpu.VMEM((n_blk, tok, BLK), F32),
-                pltpu.VMEM((n_blk, tok, BLK), F32),
-                pltpu.VMEM((tok, d), BF16),
-                dma((POOL, groups)), dma((4,)),
+                pltpu.VMEM((2, n_slots // 2, BLK), BF16),
+                pltpu.VMEM((n_big + 1, 2, 2, tok, BLK), F32),
+                pltpu.VMEM((n_big, 2, tok, BLK), F32),
+                pltpu.VMEM((n_big, 2, tok, BLK), F32),
+                pltpu.VMEM((n_big, tok, BLK), F32),
+                pltpu.VMEM((n_big, tok, BLK), F32),
+                pltpu.VMEM((n_big, tok, BLK), F32),
+                pltpu.VMEM((n_slots, LAST), BF16),
+                pltpu.VMEM((2, 2, 2, tok, LAST), F32),
+                pltpu.VMEM((2, 2, tok, LAST), F32),
+                pltpu.VMEM((2, 2, tok, LAST), F32),
+                pltpu.VMEM((2, 3, tok, LAST), F32),
+                dma((POOL, 2 * groups)), dma((4,)),
                 dma((3,)), dma((3,)), dma((3,)), dma((3,)),
-                dma((n_blk,)), dma((n_blk,)), dma((n_blk,)), dma((n_blk,)), dma((n_blk,)), dma((n_blk,)),
-                dma((n_blk,)),
+                dma((n_big,)), dma((n_big,)), dma((n_big,)), dma((n_big,)), dma((n_big,)), dma((n_big,)),
+                dma((2,)), dma((2,)), dma((2, 3)), dma((2, 3)),
             ],
             compiler_params=pltpu.CompilerParams(
-                collective_id=0, has_side_effects=True, vmem_limit_bytes=67043328),
+                collective_id=0, has_side_effects=True, vmem_limit_bytes=66500000),
             name="moe_layer",
         )(hidden, expert_ids.T, norm_w.reshape(d // 128, 128), router_w, w_gate, w_up, w_down.reshape(local * ff, d))
 

time: 63.2 us -> 61.2 us (0.968)
  Pallas kernels: 61.4 us -> 60.4 us
  local copies, waits for them, and re-layouts: 1.67 us -> 0.71 us
    pallas_call x1, Pallas kernels: 61.4 us -> 60.4 us  [per_device(): pl.pallas_call(functools.partial(moe_kernel, dims), out_shape=pltpu.VMEM(...]
    unnamed x1, local copies, waits for them, and re-layouts: 1.67 us -> 0.71 us
where the time goes in v4:
time: 61.2 us; the launch traced here: 61.1 us
  Pallas kernels  60.4 us (99%)
  local copies, waits for them, and re-layouts  0.71 us (1%)
    pallas_call x1, Pallas kernels, per_device(): pl.pallas_call(functools.partial(moe_kernel, dims), out_shape=pltpu.VMEM(...  60.4 us

profile of v4, /device:TPU:0, one launch (start us, length us, event | category | flops | bytes accessed | tf_op | source)
XLA Modules:
  0.0 61.1 jit_solution(17702406797381633073)
XLA Ops:
  0.0 60.4 %moe_layer.1 = bf16[64,2048]{1,0:T(8,128)(2,1)S(1)} custom-call(bf16[64,2048]{1,0:T(8,128)(2,1)} %h_hbm.1, s32[8,64]{1,0:T(8,128)} %bitcast.4, bf16[16,128]{1,0:T(8,128)(2,1)} %bitcast.5, bf16[2048,128]{1,0:T(8,128)(2,1)} %rw_hbm.1, bf16[32,2048,384]{2,1,0:T(8,128)(2,1)} %wg_hbm.1, bf16[32,2048,384]{2,1,0:T(8,128)(2,1)} %wu_hbm.1, bf16[12288,2048]{1,0:T(8,128)(2,1)} %bitcast.3), custom_call_target="tpu_custom_call" | custom-call | tf_op jit(solution)/shard_map/moe_layer/pallas_call | solution.py:423
  60.4 0.7 %copy.9 = bf16[64,2048]{1,0:T(8,128)(2,1)} copy(bf16[64,2048]{1,0:T(8,128)(2,1)S(1)} %moe_layer.1) | data formatting | bytes 524288

commit v5 on v4

--- a/solution.py
+++ b/solution.py
@@ -12,6 +12,7 @@
 BLK = 256
 LAST = 128
 UP_UNROLL = 2
+SEEN = 6
 F32 = jnp.float32
 BF16 = jnp.bfloat16
 
@@ -101,13 +102,17 @@
     for dev in (partner, across, other, diag):
         pl.semaphore_signal(barrier, inc=1, device_id=dev, device_id_type=MESH)
 
-    def first_chunk(i, carry):
-        for cp in up_copies(i, i):
-            cp.start()
-        return carry
-
-    lax.fori_loop(0, POOL, first_chunk, 0)
-    rw_c.start()
+    def first_chunks(lo, hi):
+        for i in range(lo, hi):
+            for cp in up_copies(i, i):
+                cp.start()
+
+    def seen_chunks(lo, hi):
+        for i in range(lo, hi):
+            for cp in up_copies(i, i):
+                cp.wait()
+
+    first_chunks(0, 3)
     own_h.wait()
     own_i.wait()
     pl.semaphore_wait(barrier, 4)
@@ -132,6 +137,8 @@
     h_x.start()
     i_p.start()
     h_p.start()
+    first_chunks(3, 4)
+    rw_c.start()
 
     nw_c.wait()
 
@@ -144,9 +151,13 @@
             vbuf[pl.ds(pl.multiple_of(q * tok, tok), tok), cols] = part.astype(BF16)
 
     norm_rows(q_own)
+    seen_chunks(0, 1)
+    first_chunks(4, 5)
     i_copy(q_partner, q_partner, partner, 1).wait_recv()
     i_x.wait_recv()
     i_r.start()
+    seen_chunks(1, 3)
+    first_chunks(5, 7)
     i_copy(q_diag, q_diag, partner, 2).wait_recv()
 
     ids_t = jnp.concatenate([idb[q] for q in range(4)], axis=1)
@@ -162,6 +173,8 @@
 
     h_copy(q_partner, q_partner, partner, 1).wait_recv()
     norm_rows(q_partner)
+    seen_chunks(3, 4)
+    first_chunks(7, 8)
 
     pos_loc = posb[pl.ds(pl.multiple_of(ep * local, local), local), :]
     rank_f = lax.broadcasted_iota(jnp.int32, (chip_rows, chip_tok), 0).astype(F32)
@@ -171,18 +184,22 @@
         pick = jnp.concatenate(
             [jnp.where(pos_chip[e:e + 1, :] == rank_f, 1.0, 0.0).astype(BF16) for e in range(local)], axis=0)
 
-        def cols_step(n, carry):
-            cols = pl.ds(pl.multiple_of(n * 256, 256), 256)
-            v_cols = vbuf[chip * chip_tok:(chip + 1) * chip_tok, cols]
-            rows = jnp.dot(pick, v_cols, preferred_element_type=F32).astype(BF16)
-            xbuf[:, chip, :, cols] = rows.reshape(local, chip_rows, 256)
+        def cols_step(i, carry):
+            for u in range(4):
+                cols = pl.ds(pl.multiple_of(i * 1024 + u * 256, 256), 256)
+                v_cols = vbuf[chip * chip_tok:(chip + 1) * chip_tok, cols]
+                rows = jnp.dot(pick, v_cols, preferred_element_type=F32).astype(BF16)
+                xbuf[:, chip, :, cols] = rows.reshape(local, chip_rows, 256)
             return carry
 
-        lax.fori_loop(0, d // 256, cols_step, 0)
+        lax.fori_loop(0, d // 1024, cols_step, 0)
 
     gather_rows(0)
+    seen_chunks(4, SEEN)
+    first_chunks(8, 10)
     h_x.wait_recv()
     h_r.start()
+    first_chunks(10, POOL)
     norm_rows(q_across)
     h_copy(q_diag, q_diag, partner, 2).wait_recv()
     norm_rows(q_diag)
@@ -190,9 +207,12 @@
 
     def gate_up(i, carry):
         first = i * UP_UNROLL
-        for u in range(UP_UNROLL):
-            for cp in up_copies(first + u, lax.rem(first + u, POOL)):
-                cp.wait()
+        @pl.when(first >= SEEN)
+        def _():
+            for u in range(UP_UNROLL):
+                for cp in up_copies(first + u, lax.rem(first + u, POOL)):
+                    cp.wait()
+
         for u in range(UP_UNROLL):
             e = first + u
             rows = pl.ds(pl.multiple_of(e * slot_rows, slot_rows), slot_rows)

time: 61.2 us -> 60.7 us (level)
  no operation moved by 1% of the time
where the time goes in v5:
time: 60.7 us; the launch traced here: 60.6 us
  Pallas kernels  59.9 us (99%)
  local copies, waits for them, and re-layouts  0.71 us (1%)
    pallas_call x1, Pallas kernels, per_device(): pl.pallas_call(functools.partial(moe_kernel, dims), out_shape=pltpu.VMEM(...  59.9 us

profile of v5, /device:TPU:0, one launch (start us, length us, event | category | flops | bytes accessed | tf_op | source)
XLA Modules:
  0.0 60.6 jit_solution(3230628039250725938)
XLA Ops:
  0.0 59.9 %moe_layer.1 = bf16[64,2048]{1,0:T(8,128)(2,1)S(1)} custom-call(bf16[64,2048]{1,0:T(8,128)(2,1)} %h_hbm.1, s32[8,64]{1,0:T(8,128)} %bitcast.4, bf16[16,128]{1,0:T(8,128)(2,1)} %bitcast.5, bf16[2048,128]{1,0:T(8,128)(2,1)} %rw_hbm.1, bf16[32,2048,384]{2,1,0:T(8,128)(2,1)} %wg_hbm.1, bf16[32,2048,384]{2,1,0:T(8,128)(2,1)} %wu_hbm.1, bf16[12288,2048]{1,0:T(8,128)(2,1)} %bitcast.3), custom_call_target="tpu_custom_call" | custom-call | tf_op jit(solution)/shard_map/moe_layer/pallas_call | solution.py:443
  59.9 0.7 %copy.9 = bf16[64,2048]{1,0:T(8,128)(2,1)} copy(bf16[64,2048]{1,0:T(8,128)(2,1)S(1)} %moe_layer.1) | data formatting | bytes 524288

commit v6 on v4

--- a/solution.py
+++ b/solution.py
@@ -9,8 +9,10 @@
 
 NORM_EPS = 1e-6
 POOL = 15
+HALVED = 5
 BLK = 256
 LAST = 128
+LANES = 128
 UP_UNROLL = 2
 F32 = jnp.float32
 BF16 = jnp.bfloat16
@@ -22,10 +24,10 @@
 
 def moe_kernel(dims, h_hbm, ids_hbm, nw_hbm, rw_hbm, wg_hbm, wu_hbm, wd_hbm, out_ref,
                pool, hbuf, idb, nwb, rwb, vbuf, xbuf, posb, cbuf, abuf, ybuf,
-               sbuf, ra, tb, rb, zb, rc, ylast, slast, ra2, tb2, r2,
+               sbuf, ra, tb, rb, zb, rc, ob, og, ylast, slast, ra2, tb2, z2, r2,
                wsem, lsem, hs_sem, hr_sem, is_sem, ir_sem,
                as_sem, ar_sem, bs_sem, br_sem, cs_sem, cr_sem,
-               as2_sem, ar2_sem, xs2_sem, xr2_sem):
+               es_sem, er_sem, as2_sem, ar2_sem, xs2_sem, xr2_sem):
     tok, top_k, n_exp, local, ff, d, cap = dims
     n_tok = 4 * tok
     chip_tok = 2 * tok
@@ -44,7 +46,7 @@
     partner = {"ep": x * 2 + (1 - core)}
     across = {"ep": (1 - x) * 2 + core}
     other = {"tp": 1 - lax.axis_index("tp")}
-    diag = {**other, **across}
+    tp = lax.axis_index("tp")
     MESH = pl.DeviceIdType.MESH
     q_own, q_partner = core, 1 - core
     q_across, q_diag = 2 + core, 3 - core
@@ -96,21 +98,18 @@
     own_h.start()
     own_i.start()
     nw_c.start()
+    rw_c.start()
 
     barrier = pltpu.get_barrier_semaphore()
-    for dev in (partner, across, other, diag):
+    for dev in (partner, across, other):
         pl.semaphore_signal(barrier, inc=1, device_id=dev, device_id_type=MESH)
 
-    def first_chunk(i, carry):
+    for i in range(POOL):
         for cp in up_copies(i, i):
             cp.start()
-        return carry
-
-    lax.fori_loop(0, POOL, first_chunk, 0)
-    rw_c.start()
     own_h.wait()
     own_i.wait()
-    pl.semaphore_wait(barrier, 4)
+    pl.semaphore_wait(barrier, 3)
 
     def h_copy(q, dst, dev, n):
         return pltpu.make_async_remote_copy(
@@ -171,22 +170,48 @@
         pick = jnp.concatenate(
             [jnp.where(pos_chip[e:e + 1, :] == rank_f, 1.0, 0.0).astype(BF16) for e in range(local)], axis=0)
 
-        def cols_step(n, carry):
-            cols = pl.ds(pl.multiple_of(n * 256, 256), 256)
-            v_cols = vbuf[chip * chip_tok:(chip + 1) * chip_tok, cols]
-            rows = jnp.dot(pick, v_cols, preferred_element_type=F32).astype(BF16)
-            xbuf[:, chip, :, cols] = rows.reshape(local, chip_rows, 256)
+        def cols_step(i, carry):
+            for u in range(4):
+                cols = pl.ds(pl.multiple_of(i * 1024 + u * 256, 256), 256)
+                v_cols = vbuf[chip * chip_tok:(chip + 1) * chip_tok, cols]
+                rows = jnp.dot(pick, v_cols, preferred_element_type=F32).astype(BF16)
+                xbuf[:, chip, :, cols] = rows.reshape(local, chip_rows, 256)
             return carry
 
-        lax.fori_loop(0, d // 256, cols_step, 0)
+        lax.fori_loop(0, d // 1024, cols_step, 0)
+
+    def router(chip):
+        toks = slice(chip * chip_tok, (chip + 1) * chip_tok)
+        logits = jnp.dot(vbuf[toks, :], rwb[...], preferred_element_type=F32)
+        expo = jnp.exp(logits - jnp.max(logits, axis=-1, keepdims=True))
+        prob = expo / jnp.sum(expo, axis=-1, keepdims=True)
+        g_hi = prob.astype(BF16)
+        rest = prob - g_hi.astype(F32)
+        g_mid = rest.astype(BF16)
+        g_lo = (rest - g_mid.astype(F32)).astype(BF16)
+        pos_t = posb[:, toks].T.astype(BF16)
+        n_cols = per * chip_rows
+        for h in range(n_half):
+            lane = lax.broadcasted_iota(jnp.int32, (n_exp, n_cols), 1)
+            sub = lax.broadcasted_iota(jnp.int32, (n_exp, n_cols), 0)
+            spread = jnp.where(sub == ep * local + h * per + lane // chip_rows, 1.0, 0.0).astype(BF16)
+            want = (lax.broadcasted_iota(jnp.int32, (chip_tok, n_cols), 1) % chip_rows).astype(F32)
+            hit = jnp.dot(pos_t, spread, preferred_element_type=F32) == want
+            for i, g in enumerate((g_hi, g_mid, g_lo)):
+                wide_g = jnp.dot(g, spread, preferred_element_type=F32)
+                cbuf[h, chip, i * chip_tok:(i + 1) * chip_tok, :] = jnp.where(hit, wide_g, 0.0).astype(BF16)
 
     gather_rows(0)
+    rw_c.wait()
+    router(0)
     h_x.wait_recv()
     h_r.start()
     norm_rows(q_across)
     h_copy(q_diag, q_diag, partner, 2).wait_recv()
     norm_rows(q_diag)
     gather_rows(1)
+
+    trips = local // UP_UNROLL
 
     def gate_up(i, carry):
         first = i * UP_UNROLL
@@ -201,38 +226,18 @@
             abuf[rows, :] = (gate * jax.nn.sigmoid(gate) * up).astype(BF16)
         for u in range(UP_UNROLL):
             start_chunk(first + u + POOL)
+
+        @pl.when(i == trips // 2)
+        def _():
+            router(1)
         return carry
 
-    trips = local // UP_UNROLL
-    lax.fori_loop(0, trips // 2, gate_up, 0)
-
-    rw_c.wait()
-    logits = jnp.dot(vbuf[...], rwb[...], preferred_element_type=F32)
-    expo = jnp.exp(logits - jnp.max(logits, axis=-1, keepdims=True))
-    prob = expo / jnp.sum(expo, axis=-1, keepdims=True)
-    g_hi = prob.astype(BF16)
-    rest = prob - g_hi.astype(F32)
-    g_mid = rest.astype(BF16)
-    g_lo = (rest - g_mid.astype(F32)).astype(BF16)
-    chip_of = lax.broadcasted_iota(jnp.int32, (n_exp, n_tok), 1) // chip_tok
-    pos_all = posb[...]
-    pos_all = jnp.where(pos_all < 0.0, -1.0, pos_all + (chip_of * chip_rows).astype(F32))
-    pos_t = pos_all.T.astype(BF16)
-    for n in range(n_slots // 256):
-        lane = lax.broadcasted_iota(jnp.int32, (n_exp, 256), 1) + n * 256
-        sub = lax.broadcasted_iota(jnp.int32, (n_exp, 256), 0)
-        spread = jnp.where(sub == ep * local + lane // slot_rows, 1.0, 0.0).astype(BF16)
-        want = (lax.broadcasted_iota(jnp.int32, (n_tok, 256), 1) % slot_rows).astype(F32)
-        hit = jnp.dot(pos_t, spread, preferred_element_type=F32) == want
-        for i, g in enumerate((g_hi, g_mid, g_lo)):
-            wide_g = jnp.dot(g, spread, preferred_element_type=F32)
-            cbuf[i, :, n * 256:(n + 1) * 256] = jnp.where(hit, wide_g, 0.0).astype(BF16)
-
-    lax.fori_loop(trips // 2, trips, gate_up, 0)
+    lax.fori_loop(0, trips, gate_up, 0)
+
 
     def a_copy(c):
         return pltpu.make_async_remote_copy(
-            src_ref=sbuf.at[c + 1, :, 1 - core], dst_ref=ra.at[c],
+            src_ref=sbuf.at[c, :, 1 - core], dst_ref=ra.at[c],
             send_sem=as_sem.at[c], recv_sem=ar_sem.at[c], device_id=partner, device_id_type=MESH)
 
     def b_copy(c):
@@ -245,45 +250,83 @@
             src_ref=zb.at[c], dst_ref=rc.at[c],
             send_sem=cs_sem.at[c], recv_sem=cr_sem.at[c], device_id=other, device_id_type=MESH)
 
+    def c_half_copy(c):
+        return pltpu.make_async_remote_copy(
+            src_ref=zb.at[c, 1 - tp], dst_ref=rc.at[c, 0],
+            send_sem=cs_sem.at[c], recv_sem=cr_sem.at[c], device_id=other, device_id_type=MESH)
+
+    def e_copy(c):
+        return pltpu.make_async_remote_copy(
+            src_ref=ob.at[c], dst_ref=og.at[c],
+            send_sem=es_sem.at[c], recv_sem=er_sem.at[c], device_id=other, device_id_type=MESH)
+
     def stage_b(c):
         a_copy(c).wait_recv()
-        tb[c] = sbuf[c + 1, :, core] + ra[c]
+        tb[c] = sbuf[c, :, core] + ra[c]
         b_copy(c).start()
 
+    def sum_x(c):
+        b_copy(c).wait_recv()
+        z = tb[c, 0] + rb[c]
+        for n in range(2):
+            zb[c, n] = z[:, n * LANES:(n + 1) * LANES]
+
+    def stage_c_half(c):
+        sum_x(c)
+        c_half_copy(c).start()
+
     def stage_c(c):
-        b_copy(c).wait_recv()
-        zb[c] = tb[c, 0] + rb[c]
+        sum_x(c)
         c_copy(c).start()
+
+    def half_cols(c, n):
+        return pl.ds(pl.multiple_of(c * BLK + n * LANES, LANES), LANES)
+
+    def stage_d_half(c):
+        c_half_copy(c).wait_recv()
+        ob[c] = (hbuf[q_own, :, half_cols(c, tp)].astype(F32) + (zb[c, tp] + rc[c, 0])).astype(BF16)
+        e_copy(c).start()
+        out_ref[:, half_cols(c, tp)] = ob[c]
+
+    def stage_e(c):
+        e_copy(c).wait_recv()
+        out_ref[:, half_cols(c, 1 - tp)] = og[c]
 
     def stage_d(c):
         c_copy(c).wait_recv()
-        cols = pl.ds(pl.multiple_of(c * BLK, BLK), BLK)
-        out_ref[:, cols] = (hbuf[q_own, :, cols].astype(F32) + (zb[c] + rc[c])).astype(BF16)
+        for n in range(2):
+            cols = half_cols(c, n)
+            out_ref[:, cols] = (hbuf[q_own, :, cols].astype(F32) + (zb[c, n] + rc[c, n])).astype(BF16)
 
     def a2_copy(f):
         return pltpu.make_async_remote_copy(
             src_ref=slast.at[f, :, 1 - core], dst_ref=ra2.at[f],
             send_sem=as2_sem.at[f], recv_sem=ar2_sem.at[f], device_id=partner, device_id_type=MESH)
 
-    def x2_copies(f):
-        return [
-            pltpu.make_async_remote_copy(
-                src_ref=tb2.at[f, src], dst_ref=r2.at[f, n],
-                send_sem=xs2_sem.at[f, n], recv_sem=xr2_sem.at[f, n], device_id=dev, device_id_type=MESH)
-            for n, (src, dev) in enumerate(((1, diag), (1, across), (0, other)))]
-
-    def stage_x2(f):
+    def x2_copy(f):
+        return pltpu.make_async_remote_copy(
+            src_ref=tb2.at[f, 1], dst_ref=r2.at[f, 0],
+            send_sem=xs2_sem.at[f, 0], recv_sem=xr2_sem.at[f, 0], device_id=across, device_id_type=MESH)
+
+    def y2_copy(f):
+        return pltpu.make_async_remote_copy(
+            src_ref=z2.at[f], dst_ref=r2.at[f, 1],
+            send_sem=xs2_sem.at[f, 1], recv_sem=xr2_sem.at[f, 1], device_id=other, device_id_type=MESH)
+
+    def stage_b2(f):
         a2_copy(f).wait_recv()
         tb2[f] = slast[f, :, core] + ra2[f]
-        for cp in x2_copies(f):
-            cp.start()
+        x2_copy(f).start()
+
+    def stage_c2(f):
+        x2_copy(f).wait_recv()
+        z2[f] = tb2[f, 0] + r2[f, 0]
+        y2_copy(f).start()
 
     def stage_d2(f):
-        for cp in x2_copies(f):
-            cp.wait_recv()
+        y2_copy(f).wait_recv()
         cols = pl.ds(n_big * BLK + f * LAST, LAST)
-        moe = (tb2[f, 0] + r2[f, 1]) + (r2[f, 2] + r2[f, 0])
-        out_ref[:, cols] = (hbuf[q_own, :, cols].astype(F32) + moe).astype(BF16)
+        out_ref[:, cols] = (hbuf[q_own, :, cols].astype(F32) + (z2[f] + r2[f, 1])).astype(BF16)
 
     def act_rows(e):
         return abuf[e * slot_rows:(e + 1) * slot_rows, :]
@@ -304,7 +347,9 @@
                 part = jnp.dot(act[:, lo:lo + size], pool[slot, row:row + size, g * BLK:(g + 1) * BLK],
                                preferred_element_type=F32)
                 y = part if y is None else y + part
-            ybuf[h, k * slot_rows:(k + 1) * slot_rows, :] = y.astype(BF16)
+            y = y.astype(BF16)
+            for chip in range(2):
+                ybuf[h, chip, k * chip_rows:(k + 1) * chip_rows, :] = y[chip * chip_rows:(chip + 1) * chip_rows]
 
     def down_last(slot):
         for k in range(per):
@@ -314,20 +359,26 @@
                 part = jnp.dot(act[:, lo:lo + size], pool[slot, row:row + size, g * BLK:(g + 1) * BLK],
                                preferred_element_type=F32)
                 y = part if y is None else y + part
+            y = y.astype(BF16)
             for h in range(n_half):
-                e = h * per + k
-                ylast[e * slot_rows:(e + 1) * slot_rows, :] = (
-                    y[h * slot_rows:(h + 1) * slot_rows, h * LAST:(h + 1) * LAST].astype(BF16))
-
-    def combine(y_all, slots):
-        total = jnp.dot(cbuf[2, :, slots], y_all, preferred_element_type=F32)
-        total = total + jnp.dot(cbuf[1, :, slots], y_all, preferred_element_type=F32)
-        return total + jnp.dot(cbuf[0, :, slots], y_all, preferred_element_type=F32)
-
-    half_slots = per * slot_rows
+                for chip in range(2):
+                    row = h * slot_rows + chip * chip_rows
+                    ylast[h, chip, k * chip_rows:(k + 1) * chip_rows, :] = y[row:row + chip_rows, h * LAST:(h + 1) * LAST]
+
+    def combine(parts):
+        sums = []
+        for chip in range(2):
+            lhs = jnp.concatenate([cbuf[h, chip] for h, _ in parts], axis=1)
+            rhs = jnp.concatenate([y[h, chip] for h, y in parts], axis=0)
+            wide = jnp.dot(lhs, rhs, preferred_element_type=F32)
+            sums.append(wide[2 * chip_tok:] + wide[chip_tok:2 * chip_tok] + wide[:chip_tok])
+        return jnp.stack(sums).reshape(2, 2, tok, -1)
 
     def combine_half(h):
-        return combine(ybuf[h], pl.ds(h * half_slots, half_slots)).reshape(2, 2, tok, BLK)
+        return combine([(h, ybuf)])
+
+    def combine_last():
+        return combine([(h, ylast) for h in range(n_half)])
 
     def wait_down(j):
         slot = lax.rem(local + j, POOL)
@@ -338,72 +389,74 @@
     def down(c, carry):
         slot = wait_down(2 * c)
         down_half(slot, 0)
-        sbuf[c] += combine_half(1)
-        start_chunk(local + 2 * c + POOL)
-
-        @pl.when(c >= 1)
-        def _():
-            a_copy(c - 1).start()
-
-        for lag, stage in ((2, stage_b), (4, stage_c), (6, stage_d)):
-            @pl.when(c >= lag)
-            def _(lag=lag, stage=stage):
-                stage(c - lag)
+
+        @pl.when(c == 0)
+        def _():
+            start_chunk(local + POOL)
+
+        @pl.when(c >= 4)
+        def _():
+            stage_c_half(c - 4)
 
         slot = wait_down(2 * c + 1)
         down_half(slot, 1)
-        sbuf[c + 1] = combine_half(0)
-        start_chunk(local + 2 * c + 1 + POOL)
+        sbuf[c] = combine_half(0)
+        sbuf[c] += combine_half(1)
+        a_copy(c).start()
+
+        @pl.when(c >= 1)
+        def _():
+            stage_b(c - 1)
         return carry
 
     lax.fori_loop(0, n_big, down, 0)
 
-    all_slots = pl.ds(0, n_slots)
-    slot = (n_chunks - 2) % POOL
-    for cp in last_copies(0, slot):
-        cp.wait()
-    down_last(slot)
-    sbuf[n_big] += combine_half(1)
-    a_copy(n_big - 1).start()
-    stage_b(n_big - 2)
-    stage_c(n_big - 4)
-    slast[0] = combine(ylast[...], all_slots).reshape(2, 2, tok, LAST)
-    a2_copy(0).start()
-    slot = (n_chunks - 1) % POOL
-    for cp in last_copies(1, slot):
-        cp.wait()
-    down_last(slot)
-    slast[1] = combine(ylast[...], all_slots).reshape(2, 2, tok, LAST)
-    a2_copy(1).start()
-    stage_b(n_big - 1)
-    stage_c(n_big - 3)
-    stage_x2(0)
-    stage_x2(1)
-    stage_d(n_big - 6)
-    stage_c(n_big - 2)
-    stage_d(n_big - 5)
-    stage_d(n_big - 4)
-    stage_c(n_big - 1)
-    stage_d(n_big - 3)
+    def last_block(f):
+        slot = (n_wide + f) % POOL
+        for cp in last_copies(f, slot):
+            cp.wait()
+        down_last(slot)
+        slast[f] = combine_last()
+        a2_copy(f).start()
+
+    last_block(0)
+    stage_c_half(3)
+    stage_b(6)
+    stage_d_half(0)
+    last_block(1)
+    stage_b2(0)
+    stage_c_half(4)
+    stage_b2(1)
+    stage_d_half(1)
+    stage_c(5)
+    stage_d_half(2)
+    stage_c(6)
+    stage_d_half(3)
+    stage_c2(0)
+    stage_c2(1)
+    stage_d_half(4)
+    for c in range(HALVED):
+        stage_e(c)
+    stage_d(5)
+    stage_d(6)
     stage_d2(0)
-    stage_d(n_big - 2)
     stage_d2(1)
-    stage_d(n_big - 1)
 
     for cp in (i_x, i_p, i_r, h_x, h_p, h_r):
         cp.wait_send()
 
-    def drain(c, carry):
+    for c in range(n_big):
         a_copy(c).wait_send()
         b_copy(c).wait_send()
-        c_copy(c).wait_send()
-        return carry
-
-    lax.fori_loop(0, n_big, drain, 0)
+        if c < HALVED:
+            c_half_copy(c).wait_send()
+            e_copy(c).wait_send()
+        else:
+            c_copy(c).wait_send()
     for f in range(2):
         a2_copy(f).wait_send()
-        for cp in x2_copies(f):
-            cp.wait_send()
+        x2_copy(f).wait_send()
+        y2_copy(f).wait_send()
 
 
 def solution(mesh):
@@ -434,24 +487,27 @@
                 pltpu.VMEM((n_tok, d), BF16),
                 pltpu.VMEM((local, 2, 2 * cap, d), BF16),
                 pltpu.VMEM((n_exp, n_tok), F32),
-                pltpu.VMEM((3, n_tok, n_slots), BF16),
+                pltpu.VMEM((2, 2, 3 * n_tok // 2, n_slots // 4), BF16),
                 pltpu.VMEM((n_slots, ff), BF16),
-                pltpu.VMEM((2, n_slots // 2, BLK), BF16),
-                pltpu.VMEM((n_big + 1, 2, 2, tok, BLK), F32),
+                pltpu.VMEM((2, 2, n_slots // 4, BLK), BF16),
+                pltpu.VMEM((n_big, 2, 2, tok, BLK), F32),
                 pltpu.VMEM((n_big, 2, tok, BLK), F32),
                 pltpu.VMEM((n_big, 2, tok, BLK), F32),
                 pltpu.VMEM((n_big, tok, BLK), F32),
-                pltpu.VMEM((n_big, tok, BLK), F32),
-                pltpu.VMEM((n_big, tok, BLK), F32),
-                pltpu.VMEM((n_slots, LAST), BF16),
+                pltpu.VMEM((n_big, 2, tok, LANES), F32),
+                pltpu.VMEM((n_big, 2, tok, LANES), F32),
+                pltpu.VMEM((HALVED, tok, LANES), BF16),
+                pltpu.VMEM((HALVED, tok, LANES), BF16),
+                pltpu.VMEM((2, 2, n_slots // 4, LAST), BF16),
                 pltpu.VMEM((2, 2, 2, tok, LAST), F32),
                 pltpu.VMEM((2, 2, tok, LAST), F32),
                 pltpu.VMEM((2, 2, tok, LAST), F32),
-                pltpu.VMEM((2, 3, tok, LAST), F32),
+                pltpu.VMEM((2, tok, LAST), F32),
+                pltpu.VMEM((2, 2, tok, LAST), F32),
                 dma((POOL, 2 * groups)), dma((4,)),
                 dma((3,)), dma((3,)), dma((3,)), dma((3,)),
                 dma((n_big,)), dma((n_big,)), dma((n_big,)), dma((n_big,)), dma((n_big,)), dma((n_big,)),
-                dma((2,)), dma((2,)), dma((2, 3)), dma((2, 3)),
+                dma((HALVED,)), dma((HALVED,)), dma((2,)), dma((2,)), dma((2, 2)), dma((2, 2)),
             ],
             compiler_params=pltpu.CompilerParams(
                 collective_id=0, has_side_effects=True, vmem_limit_bytes=66500000),

time: 61.2 us -> 59.9 us (0.979)
  Pallas kernels: 60.4 us -> 59.1 us
    pallas_call x1, Pallas kernels: 60.4 us -> 59.1 us  [per_device(): pl.pallas_call(functools.partial(moe_kernel, dims), out_shape=pltpu.VMEM(...]
where the time goes in v6:
time: 59.9 us; the launch traced here: 59.8 us
  Pallas kernels  59.1 us (99%)
  local copies, waits for them, and re-layouts  0.71 us (1%)
    pallas_call x1, Pallas kernels, per_device(): pl.pallas_call(functools.partial(moe_kernel, dims), out_shape=pltpu.VMEM(...  59.1 us

profile of v6, /device:TPU:0, one launch (start us, length us, event | category | flops | bytes accessed | tf_op | source)
XLA Modules:
  0.0 59.8 jit_solution(7332707343606902643)
XLA Ops:
  0.0 59.1 %moe_layer.1 = bf16[64,2048]{1,0:T(8,128)(2,1)S(1)} custom-call(bf16[64,2048]{1,0:T(8,128)(2,1)} %h_hbm.1, s32[8,64]{1,0:T(8,128)} %bitcast.4, bf16[16,128]{1,0:T(8,128)(2,1)} %bitcast.5, bf16[2048,128]{1,0:T(8,128)(2,1)} %rw_hbm.1, bf16[32,2048,384]{2,1,0:T(8,128)(2,1)} %wg_hbm.1, bf16[32,2048,384]{2,1,0:T(8,128)(2,1)} %wu_hbm.1, bf16[12288,2048]{1,0:T(8,128)(2,1)} %bitcast.3), custom_call_target="tpu_custom_call" | custom-call | tf_op jit(solution)/shard_map/moe_layer/pallas_call | solution.py:476
  59.1 0.7 %copy.9 = bf16[64,2048]{1,0:T(8,128)(2,1)} copy(bf16[64,2048]{1,0:T(8,128)(2,1)S(1)} %moe_layer.1) | data formatting | bytes 524288

commit v7 on v6

--- a/solution.py
+++ b/solution.py
@@ -394,9 +394,9 @@
         def _():
             start_chunk(local + POOL)
 
-        @pl.when(c >= 4)
-        def _():
-            stage_c_half(c - 4)
+        @pl.when(c >= 2)
+        def _():
+            stage_b(c - 2)
 
         slot = wait_down(2 * c + 1)
         down_half(slot, 1)
@@ -404,9 +404,9 @@
         sbuf[c] += combine_half(1)
         a_copy(c).start()
 
-        @pl.when(c >= 1)
-        def _():
-            stage_b(c - 1)
+        @pl.when(c >= 4)
+        def _():
+            stage_c_half(c - 4)
         return carry
 
     lax.fori_loop(0, n_big, down, 0)
@@ -420,8 +420,9 @@
         a2_copy(f).start()
 
     last_block(0)
+    stage_b(5)
+    stage_b(6)
     stage_c_half(3)
-    stage_b(6)
     stage_d_half(0)
     last_block(1)
     stage_b2(0)

time: 59.9 us -> 60.6 us (1.012)
  Pallas kernels: 59.1 us -> 59.8 us
    pallas_call x1, Pallas kernels: 59.1 us -> 59.8 us  [per_device(): pl.pallas_call(functools.partial(moe_kernel, dims), out_shape=pltpu.VMEM(...]
where the time goes in v7:
time: 60.6 us; the launch traced here: 60.5 us
  Pallas kernels  59.8 us (99%)
  local copies, waits for them, and re-layouts  0.71 us (1%)
    pallas_call x1, Pallas kernels, per_device(): pl.pallas_call(functools.partial(moe_kernel, dims), out_shape=pltpu.VMEM(...  59.8 us

profile of v7, /device:TPU:0, one launch (start us, length us, event | category | flops | bytes accessed | tf_op | source)
XLA Modules:
  0.0 60.5 jit_solution(2875109224921048356)
XLA Ops:
  0.0 59.8 %moe_layer.1 = bf16[64,2048]{1,0:T(8,128)(2,1)S(1)} custom-call(bf16[64,2048]{1,0:T(8,128)(2,1)} %h_hbm.1, s32[8,64]{1,0:T(8,128)} %bitcast.4, bf16[16,128]{1,0:T(8,128)(2,1)} %bitcast.5, bf16[2048,128]{1,0:T(8,128)(2,1)} %rw_hbm.1, bf16[32,2048,384]{2,1,0:T(8,128)(2,1)} %wg_hbm.1, bf16[32,2048,384]{2,1,0:T(8,128)(2,1)} %wu_hbm.1, bf16[12288,2048]{1,0:T(8,128)(2,1)} %bitcast.3), custom_call_target="tpu_custom_call" | custom-call | tf_op jit(solution)/shard_map/moe_layer/pallas_call | solution.py:477
  59.8 0.7 %copy.9 = bf16[64,2048]{1,0:T(8,128)(2,1)} copy(bf16[64,2048]{1,0:T(8,128)(2,1)S(1)} %moe_layer.1) | data formatting | bytes 524288
